TPU v7x, 128 devices: a whole 4x4x4 slice. The times are simulated.
128 devices in a mesh: patch: 32 (over y, z, core), hidden: 4 (over x).
Axes of the slice: x: 4, y: 4, z: 4, core: 2. Of those that a mesh axis runs over, the one named last changes fastest.
Arguments:
- nodes: bfloat16 [65536, 512], P('patch', 'hidden'), may hold values from -6 to 6
- edges: bfloat16 [262144, 512], P(('patch', 'hidden')), may hold values from -6 to 6
- senders: int32 [262144], P(('patch', 'hidden')), may hold values from 0 to 4351
- receivers: int32 [262144], P(('patch', 'hidden')), may hold values from 0 to 2047
- halo_rows: int32 [32, 2, 1024], P('patch'), may hold values from 0 to 2047
- coarse_rows: int32 [32, 32, 8], P('patch'), may hold values from 0 to 63
- edge_count: int32 [128], P(('patch', 'hidden')), may hold values from 1024 to 2048, as said below
- w_edge_in: bfloat16 [1536, 512], replicated, may hold values from -0.15625 to 0.15625
- b_edge_in: float32 [512], replicated, may hold values from -3 to 3
- w_edge_out: bfloat16 [512, 512], replicated, may hold values from -0.25 to 0.25
- b_edge_out: float32 [512], replicated, may hold values from -2 to 2
- edge_gain: float32 [512], replicated, may hold values from 0.5 to 1.5
- edge_shift: float32 [512], replicated, may hold values from -1 to 1
- w_node_in: bfloat16 [1024, 512], replicated, may hold values from -0.1875 to 0.1875
- b_node_in: float32 [512], replicated, may hold values from -3 to 3
- w_node_out: bfloat16 [512, 512], replicated, may hold values from -0.25 to 0.25
- b_node_out: float32 [512], replicated, may hold values from -2 to 2
- node_gain: float32 [512], replicated, may hold values from 0.5 to 1.5
- node_shift: float32 [512], replicated, may hold values from -1 to 1
Outputs:
- nodes_out: bfloat16 [65536, 512], P('patch', 'hidden')
- edges_out: bfloat16 [262144, 512], P(('patch', 'hidden'))
Inputs may be any that keep to these rules, and one draw needn't show every extreme that they name: `edge_count`: some block holds 2048 live edges.
All inputs are finite; a program needn't handle non-finite values.
Results may differ from a plain program's by a relative error of at most 0.007.
Values may be sent and summed in bfloat16 or wider, within the bound.
A program may use at most 128 MiB of HBM per device.

v0:
```python
import jax
import jax.numpy as jnp
from jax import lax
from jax.sharding import PartitionSpec as P

COARSE_DEV = 64


layer_epsilon = 1e-05


def in_order(blocks, dim):
    lengths = list(blocks.shape[1:])
    lengths[dim] *= blocks.shape[0]
    return jnp.moveaxis(blocks, 0, dim).reshape(lengths)


def from_everyone(array, axis):
    count = lax.axis_size(axis)
    return lax.all_to_all(
        jnp.broadcast_to(array[None], (count, *array.shape)), axis, 0, 0, tiled=True
    )


def collect(array, axis, dim):
    return in_order(from_everyone(array, axis), dim)


def extended(block, sides, width):
    for axis, dim in sides:
        count = lax.axis_size(axis)
        forward = [(i, i + 1) for i in range(count - 1)]
        forward.append((count - 1, 0))
        backward = [(target, source) for source, target in forward]
        low = lax.ppermute(
            lax.slice_in_dim(block, block.shape[dim] - width, None, axis=dim), axis, forward
        )
        high = lax.ppermute(lax.slice_in_dim(block, 0, width, axis=dim), axis, backward)
        block = jnp.concatenate([low, block, high], axis=dim)
    return block


def in_blocks(array, dim, count):
    lengths = array.shape
    blocks = array.reshape(*lengths[:dim], count, lengths[dim] // count, *lengths[dim + 1 :])
    return jnp.moveaxis(blocks, dim, 0)


def sent_and_summed(array, axis, dim):
    blocks = in_blocks(array, dim, lax.axis_size(axis))
    arrived = lax.all_to_all(blocks, axis, split_axis=0, concat_axis=0, tiled=True)
    return arrived.astype(jnp.float32).sum(axis=0)


def normalize(output, norm_gain, norm_shift):
    row_mean = jnp.mean(output, axis=1, keepdims=True)
    row_var = jnp.mean(jnp.square(output - row_mean), axis=1, keepdims=True)
    return (output - row_mean) * lax.rsqrt(row_var + layer_epsilon) * norm_gain + norm_shift


def local(
    nodes,
    edges,
    senders,
    receivers,
    halo_rows,
    coarse_rows,
    edge_count,
    w_edge_in,
    b_edge_in,
    w_edge_out,
    b_edge_out,
    edge_gain,
    edge_shift,
    w_node_in,
    b_node_in,
    w_node_out,
    b_node_out,
    node_gain,
    node_shift,
):
    own_block = collect(nodes, "hidden", 1)
    node_rows = own_block.shape[0]
    columns = own_block.shape[1]
    border_rows = halo_rows.shape[2]
    patches = lax.axis_size("patch")
    outgoing = jnp.concatenate([own_block[halo_rows[0, 0]], own_block[halo_rows[0, 1]]], axis=0)
    bordered = extended(outgoing, (("patch", 0),), border_rows)
    everyone = collect(own_block[:COARSE_DEV], "patch", 0)
    owner_start = jnp.arange(patches, dtype=jnp.int32)[:, None] * COARSE_DEV
    distant = everyone[(owner_start + coarse_rows[0]).reshape(-1)]
    sender_table = jnp.concatenate(
        [own_block, bordered[:border_rows], bordered[3 * border_rows :], distant], axis=0
    )
    live_count = edge_count[0]
    edge_rows = edges.shape[0]
    block_rows = 512
    weight_self = w_edge_in[:columns]
    weight_send = w_edge_in[columns : 2 * columns]
    weight_target = w_edge_in[2 * columns :]
    node_index = jnp.arange(node_rows, dtype=jnp.int32)

    def edge_block(summed, position):
        offset = position * block_rows
        latent = lax.dynamic_slice_in_dim(edges, offset, block_rows, 0)
        sender_code = lax.dynamic_slice_in_dim(senders, offset, block_rows, 0)
        target = lax.dynamic_slice_in_dim(receivers, offset, block_rows, 0)
        onehot = (target[:, None] == node_index[None, :]).astype(jnp.bfloat16)
        receiver_rows = jnp.dot(onehot, own_block, preferred_element_type=jnp.float32).astype(
            jnp.bfloat16
        )
        pre_active = jnp.dot(latent, weight_self, preferred_element_type=jnp.float32)
        pre_active = pre_active + jnp.dot(
            sender_table[sender_code], weight_send, preferred_element_type=jnp.float32
        )
        pre_active = (
            pre_active
            + jnp.dot(receiver_rows, weight_target, preferred_element_type=jnp.float32)
            + b_edge_in
        )
        active = jax.nn.silu(pre_active).astype(jnp.bfloat16)
        output = jnp.dot(active, w_edge_out, preferred_element_type=jnp.float32) + b_edge_out
        update = normalize(output, edge_gain, edge_shift)
        live_mask = offset + jnp.arange(block_rows, dtype=jnp.int32) < live_count
        message = jnp.where(live_mask[:, None], update, jnp.zeros_like(update))
        new_latent = (latent.astype(jnp.float32) + message).astype(jnp.bfloat16)
        summed = summed + lax.dot_general(
            onehot,
            message.astype(jnp.bfloat16),
            (((0,), (0,)), ((), ())),
            preferred_element_type=jnp.float32,
        )
        return (summed, new_latent)

    summed, pieces = lax.scan(
        edge_block,
        jnp.zeros((node_rows, columns), jnp.float32),
        jnp.arange(edge_rows // block_rows, dtype=jnp.int32),
    )
    edges_out = pieces.reshape(edge_rows, columns)
    aggregated = sent_and_summed(summed.astype(jnp.bfloat16), "hidden", 0)
    share_rows = aggregated.shape[0]
    own_rows = lax.dynamic_slice_in_dim(
        own_block, lax.axis_index("hidden") * share_rows, share_rows, 0
    )
    pre_active = jnp.dot(own_rows, w_node_in[:columns], preferred_element_type=jnp.float32)
    pre_active = (
        pre_active
        + jnp.dot(
            aggregated.astype(jnp.bfloat16), w_node_in[columns:], preferred_element_type=jnp.float32
        )
        + b_node_in
    )
    active = jax.nn.silu(pre_active).astype(jnp.bfloat16)
    output = jnp.dot(active, w_node_out, preferred_element_type=jnp.float32) + b_node_out
    update = normalize(output, node_gain, node_shift)
    new_rows = (own_rows.astype(jnp.float32) + update).astype(jnp.bfloat16)
    nodes_out = lax.all_to_all(new_rows, "hidden", split_axis=1, concat_axis=0, tiled=True)
    return (nodes_out, edges_out)


def solution(mesh):
    return jax.shard_map(
        local,
        mesh=mesh,
        in_specs=(
            P("patch", "hidden"),
            P(("patch", "hidden"), None),
            P(("patch", "hidden")),
            P(("patch", "hidden")),
            P("patch", None, None),
            P("patch", None, None),
            P(("patch", "hidden")),
            P(),
            P(),
            P(),
            P(),
            P(),
            P(),
            P(),
            P(),
            P(),
            P(),
            P(),
            P(),
        ),
        out_specs=(P("patch", "hidden"), P(("patch", "hidden"), None)),
        check_vma=False,
    )
```

profile of v0, /device:TPU:0, one launch (start us, length us, event | category | flops | bytes accessed | tf_op | source)
XLA Modules:
  0.0 249.4 jit_solution(4125994728770208471)
XLA Ops:
  0.6 1.3 copy.33
  2.2 30.5 %all_to_all.34 = bf16[4,2048,128]{1,2,0:T(8,128)(2,1)S(1)} all-to-all(bf16[4,2048,128]{1,2,0:T(8,128)(2,1)S(1)} %broadcast_in_dim.20), channel_id=1, replica_groups=mesh['patch'=32,'hidden'=4] {'hidden'}, dimensions={0} | all-to-all | bytes 4194304 | tf_op jit(solution)/shard_map/all_to_all | solution.py:20
  32.9 1.8 broadcast_in_dim.24
  34.7 8.6 %all-to-all-start.1 = ((bf16[32,64,512]{2,1,0:T(8,128)(2,1)}), bf16[32,64,512]{2,1,0:T(8,128)(2,1)}, u32[]{:S(2)}, u32[]{:S(2)}) async-start(bf16[32,64,512]{2,1,0:T(8,128)(2,1)} %broadcast_in_dim.24), calls=%async_computation.1 | async-start | bytes 4194304 | tf_op jit(solution)/shard_map/all_to_all | solution.py:20
  43.4 2.6 %copy.34 = bf16[2048,512]{1,0:T(8,128)(2,1)} copy(bf16[2048,512]{0,1:T(8,128)(2,1)S(1)} %bitcast.52) | data formatting | bytes 4194304 | tf_op jit(solution)/shard_map/reshape | solution.py:15
  45.9 7.0 %gather_fusion.1 = bf16[1024,512]{1,0:T(8,128)(2,1)} fusion(bf16[2048,512]{1,0:T(8,128)(2,1)} %copy.34, s32[1024]{0:T(1024)S(1)} %broadcast_clamp_fusion.1), kind=kCustom, calls=%fused_computation.1 | custom fusion | bytes 2101248 | tf_op jit(solution)/shard_map/gather | solution.py:87
  52.9 2.3 copy.35
  55.4 7.0 %gather_fusion.2 = bf16[1024,512]{1,0:T(8,128)(2,1)} fusion(bf16[2048,512]{1,0:T(8,128)(2,1)} %copy.34, s32[1024]{0:T(1024)S(1)} %broadcast_clamp_fusion), kind=kCustom, calls=%fused_computation.2 | custom fusion | bytes 2101248 | tf_op jit(solution)/shard_map/gather | solution.py:87
  62.4 2.3 copy.37
  64.7 4.9 %collective-permute-start.1 = (bf16[1024,512]{0,1:T(8,128)(2,1)}, bf16[1024,512]{0,1:T(8,128)(2,1)}, u32[]{:S(2)}, u32[]{:S(2)}) collective-permute-start(bf16[1024,512]{0,1:T(8,128)(2,1)} %copy.37), channel_id=1, source_target_pairs={{4,0},{8,4},{12,8},{16,12},{20,16},{24,20},{28,24},{32,28},{36,32}... | collective-permute-start | bytes 3145736 | tf_op jit(solution)/shard_map/ppermute | solution.py:38
  69.9 2.5 %fusion.33 = (bf16[512,512]{1,0:T(8,128)(2,1)}, bf16[512,512]{1,0:T(8,128)(2,1)S(1)}, bf16[512,512]{1,0:T(8,128)(2,1)}) fusion(bf16[1536,512]{1,0:T(8,128)(2,1)} %param.28), kind=kLoop, calls=%fused_computation.64 | loop fusion | bytes 3145728 | tf_op jit(solution)/shard_map/slice | solution.py:100
  72.4 3.8 %gather_fusion.3 = bf16[256,512]{1,0:T(8,128)(2,1)} fusion(bf16[2048,512]{1,0:T(8,128)(2,1)} %bitcast.9, s32[1024]{0:T(1024)S(1)} %pad_clamp_fusion.1), kind=kCustom, calls=%fused_computation.3 | custom fusion | bytes 525312 | tf_op jit(solution)/shard_map/gather | solution.py:91
  77.3 6.2 %collective-permute-done = bf16[1024,512]{0,1:T(8,128)(2,1)} collective-permute-done((bf16[1024,512]{0,1:T(8,128)(2,1)}, bf16[1024,512]{0,1:T(8,128)(2,1)}, u32[]{:S(2)}, u32[]{:S(2)}) %collective-permute-start) | collective-permute-done | bytes 1048608 | tf_op jit(solution)/shard_map/ppermute | solution.py:35
  83.4 3.4 %pad_maximum_fusion = bf16[4352,512]{0,1:T(8,128)(2,1)} fusion(bf16[256,512]{0,1:T(8,128)(2,1)S(1)} %copy.40, bf16[1024,512]{0,1:T(8,128)(2,1)} %collective-permute-done.1, bf16[1024,512]{0,1:T(8,128)(2,1)} %collective-permute-done, bf16[2048,512]{0,1:T(8,128)(2,1)S(1)} %bitcast.53), kind=kLoop, calls=%fused_computation.39 | loop fusion | flops 17825792 | bytes 8912896 | tf_op jit(solution)/shard_map/concatenate | solution.py:92
  86.9 6.6 %copy.42 = bf16[4352,512]{1,0:T(8,128)(2,1)} copy(bf16[4352,512]{0,1:T(8,128)(2,1)} %pad_maximum_fusion) | data formatting | bytes 8912896
  93.5 102.7 %while.13 = (s32[]{:T(128)}, f32[2048,512]{1,0:T(8,128)}, bf16[4,512,512]{2,1,0:T(8,128)(2,1)}, s32[4]{0:T(128)S(1)}, s32[2048]{0:T(1024)}, /*index=5*/s32[]{:T(...) while((s32[]{:T(128)}, f32[2048,512]{1,0:T(8,128)}, ...), condition=%wide.region_3.4_spmd.clone, body=%wide.region_0.3_spmd.clone.sunk | while | flops 3233812480 | bytes 37806448 | solution.py:135
  94.9 1.1 constant_dynamic-slice_fusion.2
  97.2 4.8 %gather_fusion = bf16[512,512]{1,0:T(8,128)(2,1)S(1)} fusion(bf16[4352,512]{1,0:T(8,128)(2,1)} %get-tuple-element.408, s32[1024]{0:T(1024)S(1)} %pad_clamp_fusion.3), kind=kCustom, calls=%fused_computation.clone.clone.1 | custom fusion | bytes 1050624 | tf_op jit(solution)/shard_map/while/body/eval_jaxpr/gather | solution.py:114
  102.1 2.5 convolution_add_fusion.6
  105.3 3.8 %fusion.73 = bf16[512,512]{1,0:T(8,128)(2,1)} fusion(bf16[2048,512]{1,0:T(8,128)(2,1)} %get-tuple-element.410, s32[512]{0:T(512)S(1)} %dynamic_slice.33), kind=kOutput, calls=%fused_computation.15.clone.1 | convolution fusion | flops 1075052544 | bytes 2623488 | tf_op jit(solution)/shard_map/while/body/eval_jaxpr/dot_general | solution.py:109
  109.1 2.4 fusion.74
  113.9 3.6 %select_add_fusion.2 = f32[2048,512]{1,0:T(8,128)} fusion(f32[2048,512]{1,0:T(8,128)} %get-tuple-element.378, s32[512]{0:T(512)S(1)} %dynamic_slice.33, pred[]{:T(512)S(6)} %compare.3, f32[512,512]{0,1:T(8,128)S(1)} %get-tuple-element.353, f32[512]{0:T(512)S(1)} %get-tuple-element.416, f32[512]{0:T(512)S(1)} %get-tuple-element.415, ...), kind=kOutput, calls=%fused_computation.8.clone.1 | convolution fusion | flops 1079508992 | bytes 9447937 | tf_op jit(solution)/shard_map/while/body/eval_jaxpr/dot_general | solution.py:127
  118.9 1.1 constant_dynamic-slice_fusion.2
  121.2 4.8 %gather_fusion = bf16[512,512]{1,0:T(8,128)(2,1)S(1)} fusion(bf16[4352,512]{1,0:T(8,128)(2,1)} %get-tuple-element.408, s32[1024]{0:T(1024)S(1)} %pad_clamp_fusion.3), kind=kCustom, calls=%fused_computation.clone.clone.1 | custom fusion | bytes 1050624 | tf_op jit(solution)/shard_map/while/body/eval_jaxpr/gather | solution.py:114
  126.0 2.5 convolution_add_fusion.6
  129.3 3.8 %fusion.73 = bf16[512,512]{1,0:T(8,128)(2,1)} fusion(bf16[2048,512]{1,0:T(8,128)(2,1)} %get-tuple-element.410, s32[512]{0:T(512)S(1)} %dynamic_slice.33), kind=kOutput, calls=%fused_computation.15.clone.1 | convolution fusion | flops 1075052544 | bytes 2623488 | tf_op jit(solution)/shard_map/while/body/eval_jaxpr/dot_general | solution.py:109
  133.0 2.4 fusion.74
  137.9 5.9 %select_add_fusion.2 = f32[2048,512]{1,0:T(8,128)} fusion(f32[2048,512]{1,0:T(8,128)} %get-tuple-element.378, s32[512]{0:T(512)S(1)} %dynamic_slice.33, pred[]{:T(512)S(6)} %compare.3, f32[512,512]{0,1:T(8,128)S(1)} %get-tuple-element.353, f32[512]{0:T(512)S(1)} %get-tuple-element.416, f32[512]{0:T(512)S(1)} %get-tuple-element.415, ...), kind=kOutput, calls=%fused_computation.8.clone.1 | convolution fusion | flops 1079508992 | bytes 9447937 | tf_op jit(solution)/shard_map/while/body/eval_jaxpr/dot_general | solution.py:127
  145.1 1.1 constant_dynamic-slice_fusion.2
  147.4 4.8 %gather_fusion = bf16[512,512]{1,0:T(8,128)(2,1)S(1)} fusion(bf16[4352,512]{1,0:T(8,128)(2,1)} %get-tuple-element.408, s32[1024]{0:T(1024)S(1)} %pad_clamp_fusion.3), kind=kCustom, calls=%fused_computation.clone.clone.1 | custom fusion | bytes 1050624 | tf_op jit(solution)/shard_map/while/body/eval_jaxpr/gather | solution.py:114
  152.3 2.5 convolution_add_fusion.6
  155.5 3.8 %fusion.73 = bf16[512,512]{1,0:T(8,128)(2,1)} fusion(bf16[2048,512]{1,0:T(8,128)(2,1)} %get-tuple-element.410, s32[512]{0:T(512)S(1)} %dynamic_slice.33), kind=kOutput, calls=%fused_computation.15.clone.1 | convolution fusion | flops 1075052544 | bytes 2623488 | tf_op jit(solution)/shard_map/while/body/eval_jaxpr/dot_general | solution.py:109
  159.3 2.4 fusion.74
  164.1 5.9 %select_add_fusion.2 = f32[2048,512]{1,0:T(8,128)} fusion(f32[2048,512]{1,0:T(8,128)} %get-tuple-element.378, s32[512]{0:T(512)S(1)} %dynamic_slice.33, pred[]{:T(512)S(6)} %compare.3, f32[512,512]{0,1:T(8,128)S(1)} %get-tuple-element.353, f32[512]{0:T(512)S(1)} %get-tuple-element.416, f32[512]{0:T(512)S(1)} %get-tuple-element.415, ...), kind=kOutput, calls=%fused_computation.8.clone.1 | convolution fusion | flops 1079508992 | bytes 9447937 | tf_op jit(solution)/shard_map/while/body/eval_jaxpr/dot_general | solution.py:127
  173.6 4.8 %gather_fusion = bf16[512,512]{1,0:T(8,128)(2,1)S(1)} fusion(bf16[4352,512]{1,0:T(8,128)(2,1)} %get-tuple-element.408, s32[1024]{0:T(1024)S(1)} %pad_clamp_fusion.3), kind=kCustom, calls=%fused_computation.clone.clone.1 | custom fusion | bytes 1050624 | tf_op jit(solution)/shard_map/while/body/eval_jaxpr/gather | solution.py:114
  178.5 2.5 convolution_add_fusion.6
  181.7 3.8 %fusion.73 = bf16[512,512]{1,0:T(8,128)(2,1)} fusion(bf16[2048,512]{1,0:T(8,128)(2,1)} %get-tuple-element.410, s32[512]{0:T(512)S(1)} %dynamic_slice.33), kind=kOutput, calls=%fused_computation.15.clone.1 | convolution fusion | flops 1075052544 | bytes 2623488 | tf_op jit(solution)/shard_map/while/body/eval_jaxpr/dot_general | solution.py:109
  185.5 2.4 fusion.74
  190.3 5.9 %select_add_fusion.2 = f32[2048,512]{1,0:T(8,128)} fusion(f32[2048,512]{1,0:T(8,128)} %get-tuple-element.378, s32[512]{0:T(512)S(1)} %dynamic_slice.33, pred[]{:T(512)S(6)} %compare.3, f32[512,512]{0,1:T(8,128)S(1)} %get-tuple-element.353, f32[512]{0:T(512)S(1)} %get-tuple-element.416, f32[512]{0:T(512)S(1)} %get-tuple-element.415, ...), kind=kOutput, calls=%fused_computation.8.clone.1 | convolution fusion | flops 1079508992 | bytes 9447937 | tf_op jit(solution)/shard_map/while/body/eval_jaxpr/dot_general | solution.py:127
  196.1 3.8 %convert_element_type.31 = bf16[2048,512]{1,0:T(8,128)(2,1)} convert(f32[2048,512]{1,0:T(8,128)} %get-tuple-element.100) | non-fusion elementwise | flops 1048576 | bytes 6291456 | tf_op jit(solution)/shard_map/convert_element_type | solution.py:141
  199.9 4.6 %all-to-all-start.2 = ((bf16[4,512,512]{2,1,0:T(8,128)(2,1)}), bf16[4,512,512]{2,1,0:T(8,128)(2,1)}, u32[]{:S(2)}, u32[]{:S(2)}) async-start(bf16[4,512,512]{2,1,0:T(8,128)(2,1)} %bitcast.56), calls=%async_computation.2 | async-start | bytes 4194304 | tf_op jit(solution)/shard_map/all_to_all | solution.py:51
  204.6 2.5 %fusion.27 = f32[512,512]{1,0:T(8,128)} fusion(bf16[1024,512]{1,0:T(8,128)(2,1)} %param.34, bf16[2048,512]{0,1:T(8,128)(2,1)S(1)} %bitcast.54, s32[]{:T(128)S(6)} %select_n.45), kind=kOutput, calls=%fused_computation.49 | convolution fusion | flops 268435456 | bytes 2097156 | tf_op jit(solution)/shard_map/dot_general | solution.py:146
  207.1 22.3 %all-to-all-done.2 = bf16[4,512,512]{2,1,0:T(8,128)(2,1)} async-done(((bf16[4,512,512]{2,1,0:T(8,128)(2,1)}), bf16[4,512,512]{2,1,0:T(8,128)(2,1)}, u32[]{:S(2)}, u32[]{:S(2)}) %all-to-all-start.2) | async-done | bytes 2097184 | tf_op jit(solution)/shard_map/all_to_all | solution.py:51
  229.4 2.2 reduce_sum.48
  231.6 3.4 %fusion.34 = (f32[512]{0:T(512)S(1)}, f32[512,512]{0,1:T(8,128)}) fusion(f32[512]{0:T(512)S(1)} %copy-done.14, bf16[512,512]{1,0:T(8,128)(2,1)S(1)} %copy-done, f32[512,512]{1,0:T(8,128)} %fusion.27, bf16[512,512]{1,0:T(8,128)(2,1)S(1)} %reduce_sum.48, f32[512]{0:T(512)S(1)} %copy-done.15, bf16[1024,512]{1,0:T(8,128)(2,1)} %param.34), kind=kOutput, calls=%fused_computation.65 | convolution fusion | flops 539229696 | bytes 3676160 | tf_op jit(solution)/shard_map/dot_general | solution.py:155
  235.0 1.4 multiply_reduce_fusion.1
  236.4 1.5 add_convert_fusion.1
  237.9 10.5 %all_to_all.35 = bf16[512,4,128]{0,2,1:T(8,128)(2,1)S(1)} all-to-all(bf16[512,4,128]{0,2,1:T(8,128)(2,1)S(1)} %bitcast.57), channel_id=1, replica_groups=mesh['patch'=32,'hidden'=4] {'hidden'}, dimensions={1} | all-to-all | bytes 1048576 | tf_op jit(solution)/shard_map/all_to_all | solution.py:158
  (126 shorter events, 24.6 us)
Async XLA Ops:
  0.6 230.9 %copy-start = (bf16[512,512]{1,0:T(8,128)(2,1)S(1)}, bf16[512,512]{1,0:T(8,128)(2,1)}, u32[]{:S(2)}) copy-start(bf16[512,512]{1,0:T(8,128)(2,1)} %param.36) | copy-start | bytes 1572868
  32.7 50.7 %copy-start.1 = (bf16[4,2048,128]{1,2,0:T(8,128)(2,1)}, bf16[4,2048,128]{1,2,0:T(8,128)(2,1)S(1)}, u32[]{:S(2)}) copy-start(bf16[4,2048,128]{1,2,0:T(8,128)(2,1)S(1)} %all_to_all.34) | copy-start | bytes 6291460
  34.7 8.6 %copy-start.8 = (s32[1,2,1024]{2,1,0:T(2,128)S(1)}, s32[1,2,1024]{2,1,0:T(2,128)}, u32[]{:S(2)}) copy-start(s32[1,2,1024]{2,1,0:T(2,128)} %param.25) | copy-start | bytes 24580
  34.7 37.7 %all-to-all-start.1 = ((bf16[32,64,512]{2,1,0:T(8,128)(2,1)}), bf16[32,64,512]{2,1,0:T(8,128)(2,1)}, u32[]{:S(2)}, u32[]{:S(2)}) async-start(bf16[32,64,512]{2,1,0:T(8,128)(2,1)} %broadcast_in_dim.24), calls=%async_computation.1 | async-start | bytes 4194304 | tf_op jit(solution)/shard_map/all_to_all | solution.py:20
  55.2 28.2 %collective-permute-start = (bf16[1024,512]{0,1:T(8,128)(2,1)}, bf16[1024,512]{0,1:T(8,128)(2,1)}, u32[]{:S(2)}, u32[]{:S(2)}) collective-permute-start(bf16[1024,512]{0,1:T(8,128)(2,1)} %copy.35), channel_id=1, source_target_pairs={{0,4},{4,8},{8,12},{12,16},{16,20},{20,24},{24,28},{28,32},{32,36}... | collective-permute-start | bytes 3145736 | tf_op jit(solution)/shard_map/ppermute | solution.py:35
  62.4 7.3 %copy-start.9 = (s32[1,32,8]{1,2,0:T(8,128)S(1)}, s32[1,32,8]{1,2,0:T(8,128)}, u32[]{:S(2)}) copy-start(s32[1,32,8]{1,2,0:T(8,128)} %param.26) | copy-start | bytes 3076
  64.7 18.8 %collective-permute-start.1 = (bf16[1024,512]{0,1:T(8,128)(2,1)}, bf16[1024,512]{0,1:T(8,128)(2,1)}, u32[]{:S(2)}, u32[]{:S(2)}) collective-permute-start(bf16[1024,512]{0,1:T(8,128)(2,1)} %copy.37), channel_id=1, source_target_pairs={{4,0},{8,4},{12,8},{16,12},{20,16},{24,20},{28,24},{32,28},{36,32}... | collective-permute-start | bytes 3145736 | tf_op jit(solution)/shard_map/ppermute | solution.py:38
  86.8 6.6 %copy-start.6 = (f32[512]{0:T(512)S(1)}, f32[512]{0:T(512)}, u32[]{:S(2)}) copy-start(f32[512]{0:T(512)} %param.32) | copy-start | bytes 6148
  86.8 6.6 %copy-start.7 = (f32[512]{0:T(512)S(1)}, f32[512]{0:T(512)}, u32[]{:S(2)}) copy-start(f32[512]{0:T(512)} %param.33) | copy-start | bytes 6148
  86.8 6.6 %copy-start.12 = (f32[512]{0:T(512)S(1)}, f32[512]{0:T(512)}, u32[]{:S(2)}) copy-start(f32[512]{0:T(512)} %param.29) | copy-start | bytes 6148
  86.8 6.6 %copy-start.13 = (f32[512]{0:T(512)S(1)}, f32[512]{0:T(512)}, u32[]{:S(2)}) copy-start(f32[512]{0:T(512)} %param.31) | copy-start | bytes 6148
  93.5 8.6 %copy-start.4 = (bf16[512,512]{1,0:T(8,128)(2,1)}, bf16[512,512]{1,0:T(8,128)(2,1)S(1)}, u32[]{:S(2)}) copy-start(bf16[512,512]{1,0:T(8,128)(2,1)S(1)} %get-tuple-element.406) | copy-start | bytes 1572868 | tf_op jit(solution)/shard_map/while
  105.3 3.8 %copy-start.3 = (f32[512,512]{1,0:T(8,128)S(1)}, f32[512,512]{1,0:T(8,128)}, u32[]{:S(2)}) copy-start(f32[512,512]{1,0:T(8,128)} %convolution_add_fusion.6) | copy-start | bytes 3145732 | tf_op jit(solution)/shard_map/while
  113.9 3.6 %copy-start.5 = (bf16[512,512]{1,0:T(8,128)(2,1)S(1)}, bf16[512,512]{1,0:T(8,128)(2,1)}, u32[]{:S(2)}) copy-start(bf16[512,512]{1,0:T(8,128)(2,1)} %copy-done.4) | copy-start | bytes 1572868 | tf_op jit(solution)/shard_map/while
  117.5 8.5 %copy-start.4 = (bf16[512,512]{1,0:T(8,128)(2,1)}, bf16[512,512]{1,0:T(8,128)(2,1)S(1)}, u32[]{:S(2)}) copy-start(bf16[512,512]{1,0:T(8,128)(2,1)S(1)} %get-tuple-element.406) | copy-start | bytes 1572868 | tf_op jit(solution)/shard_map/while
  129.3 3.8 %copy-start.3 = (f32[512,512]{1,0:T(8,128)S(1)}, f32[512,512]{1,0:T(8,128)}, u32[]{:S(2)}) copy-start(f32[512,512]{1,0:T(8,128)} %convolution_add_fusion.6) | copy-start | bytes 3145732 | tf_op jit(solution)/shard_map/while
  137.8 5.9 %copy-start.5 = (bf16[512,512]{1,0:T(8,128)(2,1)S(1)}, bf16[512,512]{1,0:T(8,128)(2,1)}, u32[]{:S(2)}) copy-start(bf16[512,512]{1,0:T(8,128)(2,1)} %copy-done.4) | copy-start | bytes 1572868 | tf_op jit(solution)/shard_map/while
  143.7 8.5 %copy-start.4 = (bf16[512,512]{1,0:T(8,128)(2,1)}, bf16[512,512]{1,0:T(8,128)(2,1)S(1)}, u32[]{:S(2)}) copy-start(bf16[512,512]{1,0:T(8,128)(2,1)S(1)} %get-tuple-element.406) | copy-start | bytes 1572868 | tf_op jit(solution)/shard_map/while
  155.5 3.8 %copy-start.3 = (f32[512,512]{1,0:T(8,128)S(1)}, f32[512,512]{1,0:T(8,128)}, u32[]{:S(2)}) copy-start(f32[512,512]{1,0:T(8,128)} %convolution_add_fusion.6) | copy-start | bytes 3145732 | tf_op jit(solution)/shard_map/while
  164.1 5.9 %copy-start.5 = (bf16[512,512]{1,0:T(8,128)(2,1)S(1)}, bf16[512,512]{1,0:T(8,128)(2,1)}, u32[]{:S(2)}) copy-start(bf16[512,512]{1,0:T(8,128)(2,1)} %copy-done.4) | copy-start | bytes 1572868 | tf_op jit(solution)/shard_map/while
  169.9 8.5 %copy-start.4 = (bf16[512,512]{1,0:T(8,128)(2,1)}, bf16[512,512]{1,0:T(8,128)(2,1)S(1)}, u32[]{:S(2)}) copy-start(bf16[512,512]{1,0:T(8,128)(2,1)S(1)} %get-tuple-element.406) | copy-start | bytes 1572868 | tf_op jit(solution)/shard_map/while
  181.7 3.8 %copy-start.3 = (f32[512,512]{1,0:T(8,128)S(1)}, f32[512,512]{1,0:T(8,128)}, u32[]{:S(2)}) copy-start(f32[512,512]{1,0:T(8,128)} %convolution_add_fusion.6) | copy-start | bytes 3145732 | tf_op jit(solution)/shard_map/while
  190.3 5.9 %copy-start.5 = (bf16[512,512]{1,0:T(8,128)(2,1)S(1)}, bf16[512,512]{1,0:T(8,128)(2,1)}, u32[]{:S(2)}) copy-start(bf16[512,512]{1,0:T(8,128)(2,1)} %copy-done.4) | copy-start | bytes 1572868 | tf_op jit(solution)/shard_map/while
  199.9 4.6 %copy-start.2 = (bf16[4,2048,128]{1,2,0:T(8,128)(2,1)S(1)}, bf16[4,2048,128]{1,2,0:T(8,128)(2,1)}, u32[]{:S(2)}) copy-start(bf16[4,2048,128]{1,2,0:T(8,128)(2,1)} %copy-done.1) | copy-start | bytes 6291460
  199.9 29.4 %all-to-all-start.2 = ((bf16[4,512,512]{2,1,0:T(8,128)(2,1)}), bf16[4,512,512]{2,1,0:T(8,128)(2,1)}, u32[]{:S(2)}, u32[]{:S(2)}) async-start(bf16[4,512,512]{2,1,0:T(8,128)(2,1)} %bitcast.56), calls=%async_computation.2 | async-start | bytes 4194304 | tf_op jit(solution)/shard_map/all_to_all | solution.py:51
  204.6 27.0 %copy-start.14 = (f32[512]{0:T(512)S(1)}, f32[512]{0:T(512)}, u32[]{:S(2)}) copy-start(f32[512]{0:T(512)} %param.37) | copy-start | bytes 6148
  204.6 27.0 %copy-start.15 = (f32[512]{0:T(512)S(1)}, f32[512]{0:T(512)}, u32[]{:S(2)}) copy-start(f32[512]{0:T(512)} %param.35) | copy-start | bytes 6148
  231.6 4.8 %copy-start.10 = (f32[512]{0:T(512)S(1)}, f32[512]{0:T(512)}, u32[]{:S(2)}) copy-start(f32[512]{0:T(512)} %param.39) | copy-start | bytes 6148
  231.6 4.8 %copy-start.11 = (f32[512]{0:T(512)S(1)}, f32[512]{0:T(512)}, u32[]{:S(2)}) copy-start(f32[512]{0:T(512)} %param.38) | copy-start | bytes 6148
where the time goes:
time: 252 us; the launch traced here: 249 us
  local copies, waits for them, and re-layouts  74.5 us (30%)
  matrix products  63.2 us (25%)
  blocking collectives  41 us (16%)
  waiting for transfers between devices  28.5 us (11%)
  other arithmetic  20 us (8%)
  starting transfers between devices  18.3 us (7%)
  loops' own time  3.04 us (1%)
    all_to_all x1, blocking collectives, from_everyone(): lax.all_to_all(jnp.broadcast_to(array[None], (count, *array.shape)), axis...  30.5 us
    all_to_all x1, waiting for transfers between devices, sent_and_summed(): lax.all_to_all(blocks, axis, split_axis=0, concat_axis=0, tiled=True)  22.3 us
    dot_general x4, matrix products, edge_block(): lax.dot_general(onehot, message.astype(jnp.bfloat16), (((0,), (0,)), ((),...  21.2 us
    gather x4, local copies, waits for them, and re-layouts, edge_block(): sender_table[sender_code]  19.3 us
    dot_general x4, matrix products, edge_block(): jnp.dot(onehot, own_block, preferred_element_type=jnp.float32)  15.1 us
    all_to_all x1, blocking collectives, local(): lax.all_to_all(new_rows, 'hidden', split_axis=1, concat_axis=0, tiled=True)  10.5 us
    dot_general x4, matrix products, edge_block(): jnp.dot(sender_table[sender_code], weight_send, preferred_element_type=jn...  9.85 us
    dot_general x4, matrix products, edge_block(): jnp.dot(active, w_edge_out, preferred_element_type=jnp.float32) + b_edge_out  9.45 us
  transfers between devices with their start and end apart: 4, of which 2 were waited for; matrix products, arithmetic and copies ran while one was open for 13% of the time, Pallas kernels for 0%

commit v1 on v0

--- a/solution.py
+++ b/solution.py
@@ -1,9 +1,13 @@
 import jax
 import jax.numpy as jnp
 from jax import lax
+from jax.experimental import pallas as pl
+from jax.experimental.pallas import tpu as pltpu
 from jax.sharding import PartitionSpec as P
 
 COARSE_DEV = 64
+LANES = 128
+EDGE_BLOCK = 512
 
 
 layer_epsilon = 1e-05
@@ -54,8 +58,134 @@
 
 def normalize(output, norm_gain, norm_shift):
     row_mean = jnp.mean(output, axis=1, keepdims=True)
-    row_var = jnp.mean(jnp.square(output - row_mean), axis=1, keepdims=True)
-    return (output - row_mean) * lax.rsqrt(row_var + layer_epsilon) * norm_gain + norm_shift
+    centered = output - row_mean
+    row_var = jnp.mean(jnp.square(centered), axis=1, keepdims=True)
+    return centered * lax.rsqrt(row_var + layer_epsilon) * norm_gain + norm_shift
+
+
+def silu(v):
+    half = 0.5 * v
+    return half + half * jnp.tanh(half)
+
+
+def column_of(ids_ref, row):
+    return jnp.broadcast_to(ids_ref[pl.ds(row, 1), :], (LANES, LANES)).T
+
+
+def one_hot_rows(ids_ref, first_row, rows, out_ref):
+    width = out_ref.shape[1]
+    lane = lax.broadcasted_iota(jnp.int32, (LANES, LANES), 1)
+    for r in range(rows):
+        ids = column_of(ids_ref, first_row + r)
+        for k in range(width // LANES):
+            out_ref[r * LANES : (r + 1) * LANES, k * LANES : (k + 1) * LANES] = jnp.where(
+                ids == lane + k * LANES, 1.0, 0.0
+            ).astype(jnp.bfloat16)
+
+
+def edge_kernel(
+    count_ref,
+    table_ref,
+    edges_ref,
+    senders_ref,
+    receivers_ref,
+    w_in_ref,
+    b_in_ref,
+    w_out_ref,
+    b_out_ref,
+    gain_ref,
+    shift_ref,
+    edges_out_ref,
+    sums_ref,
+    hot_send,
+    hot_recv,
+    hot_sum,
+    joined,
+    sent,
+):
+    rows, columns = edges_ref.shape
+    node_rows = sums_ref.shape[0]
+    per = EDGE_BLOCK // LANES
+
+    def edge_block(i, carry):
+        start = pl.multiple_of(i * EDGE_BLOCK, EDGE_BLOCK)
+        here = pl.ds(start, EDGE_BLOCK)
+        one_hot_rows(senders_ref, i * per, per, hot_send)
+        one_hot_rows(receivers_ref, i * per, per, hot_recv)
+        latent = edges_ref[here, :]
+        joined[:, :columns] = latent
+        joined[:, columns : 2 * columns] = jnp.dot(
+            hot_send[...], table_ref[...], preferred_element_type=jnp.float32
+        ).astype(jnp.bfloat16)
+        joined[:, 2 * columns :] = jnp.dot(
+            hot_recv[...], table_ref[:node_rows, :], preferred_element_type=jnp.float32
+        ).astype(jnp.bfloat16)
+        pre = (
+            jnp.dot(joined[...], w_in_ref[...], preferred_element_type=jnp.float32) + b_in_ref[...]
+        )
+        active = silu(pre).astype(jnp.bfloat16)
+        output = (
+            jnp.dot(active, w_out_ref[...], preferred_element_type=jnp.float32) + b_out_ref[...]
+        )
+        update = normalize(output, gain_ref[...], shift_ref[...])
+        position = start + lax.broadcasted_iota(jnp.int32, (EDGE_BLOCK, 1), 0)
+        message = jnp.where(position < count_ref[0], update, 0.0)
+        edges_out_ref[here, :] = (latent.astype(jnp.float32) + message).astype(jnp.bfloat16)
+        sent[here, :] = message.astype(jnp.bfloat16)
+        return carry
+
+    lax.fori_loop(0, rows // EDGE_BLOCK, edge_block, 0)
+
+    share = hot_sum.shape[0]
+
+    def sum_block(j, carry):
+        start = pl.multiple_of(j * share, share)
+        node = start + lax.broadcasted_iota(jnp.int32, (share, LANES), 0)
+        for k in range(rows // LANES):
+            ids = jnp.broadcast_to(receivers_ref[k : k + 1, :], (share, LANES))
+            hot_sum[:, k * LANES : (k + 1) * LANES] = jnp.where(node == ids, 1.0, 0.0).astype(
+                jnp.bfloat16
+            )
+        sums_ref[pl.ds(start, share), :] = jnp.dot(
+            hot_sum[...], sent[...], preferred_element_type=jnp.float32
+        ).astype(jnp.bfloat16)
+        return carry
+
+    lax.fori_loop(0, node_rows // share, sum_block, 0)
+
+
+def edge_stage(table, edges, senders, receivers, edge_count, w_in, b_in, w_out, b_out, gain, shift, node_rows):
+    rows, columns = edges.shape
+    vmem = pl.BlockSpec(memory_space=pltpu.VMEM)
+    return pl.pallas_call(
+        edge_kernel,
+        out_shape=(
+            jax.ShapeDtypeStruct((rows, columns), jnp.bfloat16),
+            jax.ShapeDtypeStruct((node_rows, columns), jnp.bfloat16),
+        ),
+        in_specs=[pl.BlockSpec(memory_space=pltpu.SMEM)] + [vmem] * 10,
+        out_specs=(vmem, vmem),
+        scratch_shapes=[
+            pltpu.VMEM((EDGE_BLOCK, table.shape[0]), jnp.bfloat16),
+            pltpu.VMEM((EDGE_BLOCK, node_rows), jnp.bfloat16),
+            pltpu.VMEM((512, rows), jnp.bfloat16),
+            pltpu.VMEM((EDGE_BLOCK, 3 * columns), jnp.bfloat16),
+            pltpu.VMEM((rows, columns), jnp.bfloat16),
+        ],
+        compiler_params=pltpu.CompilerParams(vmem_limit_bytes=60 * 2**20),
+    )(
+        edge_count,
+        table,
+        edges,
+        senders.reshape(-1, LANES),
+        receivers.reshape(-1, LANES),
+        w_in,
+        b_in.reshape(1, -1),
+        w_out,
+        b_out.reshape(1, -1),
+        gain.reshape(1, -1),
+        shift.reshape(1, -1),
+    )
 
 
 def local(
@@ -92,53 +222,21 @@
     sender_table = jnp.concatenate(
         [own_block, bordered[:border_rows], bordered[3 * border_rows :], distant], axis=0
     )
-    live_count = edge_count[0]
-    edge_rows = edges.shape[0]
-    block_rows = 512
-    weight_self = w_edge_in[:columns]
-    weight_send = w_edge_in[columns : 2 * columns]
-    weight_target = w_edge_in[2 * columns :]
-    node_index = jnp.arange(node_rows, dtype=jnp.int32)
-
-    def edge_block(summed, position):
-        offset = position * block_rows
-        latent = lax.dynamic_slice_in_dim(edges, offset, block_rows, 0)
-        sender_code = lax.dynamic_slice_in_dim(senders, offset, block_rows, 0)
-        target = lax.dynamic_slice_in_dim(receivers, offset, block_rows, 0)
-        onehot = (target[:, None] == node_index[None, :]).astype(jnp.bfloat16)
-        receiver_rows = jnp.dot(onehot, own_block, preferred_element_type=jnp.float32).astype(
-            jnp.bfloat16
-        )
-        pre_active = jnp.dot(latent, weight_self, preferred_element_type=jnp.float32)
-        pre_active = pre_active + jnp.dot(
-            sender_table[sender_code], weight_send, preferred_element_type=jnp.float32
-        )
-        pre_active = (
-            pre_active
-            + jnp.dot(receiver_rows, weight_target, preferred_element_type=jnp.float32)
-            + b_edge_in
-        )
-        active = jax.nn.silu(pre_active).astype(jnp.bfloat16)
-        output = jnp.dot(active, w_edge_out, preferred_element_type=jnp.float32) + b_edge_out
-        update = normalize(output, edge_gain, edge_shift)
-        live_mask = offset + jnp.arange(block_rows, dtype=jnp.int32) < live_count
-        message = jnp.where(live_mask[:, None], update, jnp.zeros_like(update))
-        new_latent = (latent.astype(jnp.float32) + message).astype(jnp.bfloat16)
-        summed = summed + lax.dot_general(
-            onehot,
-            message.astype(jnp.bfloat16),
-            (((0,), (0,)), ((), ())),
-            preferred_element_type=jnp.float32,
-        )
-        return (summed, new_latent)
-
-    summed, pieces = lax.scan(
-        edge_block,
-        jnp.zeros((node_rows, columns), jnp.float32),
-        jnp.arange(edge_rows // block_rows, dtype=jnp.int32),
-    )
-    edges_out = pieces.reshape(edge_rows, columns)
-    aggregated = sent_and_summed(summed.astype(jnp.bfloat16), "hidden", 0)
+    edges_out, summed = edge_stage(
+        sender_table,
+        edges,
+        senders,
+        receivers,
+        edge_count,
+        w_edge_in,
+        b_edge_in,
+        w_edge_out,
+        b_edge_out,
+        edge_gain,
+        edge_shift,
+        node_rows,
+    )
+    aggregated = sent_and_summed(summed, "hidden", 0)
     share_rows = aggregated.shape[0]
     own_rows = lax.dynamic_slice_in_dim(
         own_block, lax.axis_index("hidden") * share_rows, share_rows, 0

time: 252 us -> 170 us (0.67)
  matrix products: 63.2 us -> 5.72 us
  local copies, waits for them, and re-layouts: 74.5 us -> 20.9 us
  waiting for transfers between devices: 28.5 us -> 66.2 us
  Pallas kernels: 0 us -> 31.9 us
  blocking collectives: 41 us -> 10.5 us
  other arithmetic: 20 us -> 8.74 us
  starting transfers between devices: 18.3 us -> 22.5 us
  loops' own time: 3.04 us -> 0 us
    dot_general x20 -> x0, matrix products: 57.3 us -> none  [the longest x4 21.2 us: edge_block(): lax.dot_general(onehot, message.astype(jnp.bfloat16), (((0,), (0,)), ((),...]
    all_to_all x1 -> x2, waiting for transfers between devices: 0.01 us -> 37.3 us  [from_everyone(): lax.all_to_all(jnp.broadcast_to(array[None], (count, *array.shape)), axis...]
    pallas_call x0 -> x1, Pallas kernels: none -> 31.9 us  [edge_stage(): pl.pallas_call(edge_kernel, out_shape=(jax.ShapeDtypeStruct((rows, column...]
    all_to_all x1 -> x0, blocking collectives: 30.5 us -> none  [from_everyone(): lax.all_to_all(jnp.broadcast_to(array[None], (count, *array.shape)), axis...]
    gather x4 -> x0, local copies, waits for them, and re-layouts: 19.3 us -> none  [edge_block(): sender_table[sender_code]]
    dynamic_slice x16 -> x0, local copies, waits for them, and re-layouts: 11.1 us -> none  [the longest x8 5.18 us: edge_block(): latent = lax.dynamic_slice_in_dim(edges, offset, block_rows, 0)]
    unnamed x29 -> x18, local copies, waits for them, and re-layouts: 8.04 us -> 1.17 us
    convert_element_type x2 -> x0, other arithmetic: 5.31 us -> none  [the longest x1 3.79 us: local(): aggregated = sent_and_summed(summed.astype(jnp.bfloat16), 'hidden', 0)]
  transfers between devices with their start and end apart: 4 -> 5, of which waited for: 2 -> 4; matrix products, arithmetic and copies ran while one was open for 13% -> 11% of each run, Pallas kernels for 0% -> 0%
where the time goes in v1:
time: 170 us; the launch traced here: 168 us
  waiting for transfers between devices  66.2 us (39%)
  Pallas kernels  31.9 us (19%)
  starting transfers between devices  22.5 us (13%)
  local copies, waits for them, and re-layouts  20.9 us (12%)
  blocking collectives  10.5 us (6%)
  other arithmetic  8.74 us (5%)
  matrix products  5.72 us (3%)
    all_to_all x2, waiting for transfers between devices, from_everyone(): lax.all_to_all(jnp.broadcast_to(array[None], (count, *array.shape)), axis...  37.3 us
    pallas_call x1, Pallas kernels, edge_stage(): pl.pallas_call(edge_kernel, out_shape=(jax.ShapeDtypeStruct((rows, column...  31.9 us
    all_to_all x1, waiting for transfers between devices, sent_and_summed(): lax.all_to_all(blocks, axis, split_axis=0, concat_axis=0, tiled=True)  21 us
    all_to_all x2, starting transfers between devices, from_everyone(): lax.all_to_all(jnp.broadcast_to(array[None], (count, *array.shape)), axis...  13 us
    all_to_all x1, blocking collectives, local(): lax.all_to_all(new_rows, 'hidden', split_axis=1, concat_axis=0, tiled=True)  10.5 us
    ppermute x1, waiting for transfers between devices, extended(): lax.ppermute(lax.slice_in_dim(block, block.shape[dim] - width, None, axis...  7.97 us
    gather x1, local copies, waits for them, and re-layouts, local(): own_block[halo_rows[0, 1]]  5.08 us
    gather x1, local copies, waits for them, and re-layouts, local(): own_block[halo_rows[0, 0]]  5.07 us
  transfers between devices with their start and end apart: 5, of which 4 were waited for; matrix products, arithmetic and copies ran while one was open for 11% of the time, Pallas kernels for 0%

profile of v1, /device:TPU:0, one launch (start us, length us, event | category | flops | bytes accessed | tf_op | source)
XLA Modules:
  0.0 167.9 jit_solution(5716898843446308862)
XLA Ops:
  0.6 0.0 copy-start
  0.6 2.7 %broadcast_in_dim.6 = bf16[4,2048,128]{2,1,0:T(8,128)(2,1)} broadcast(bf16[2048,128]{1,0:T(8,128)(2,1)} %param.19), dimensions={1,2} | broadcast | bytes 2621440 | tf_op jit(solution)/shard_map/broadcast_in_dim | solution.py:25
  3.3 0.0 copy-start.2
  3.3 4.5 %all-to-all-start = ((bf16[4,2048,128]{2,1,0:T(8,128)(2,1)}), bf16[4,2048,128]{2,1,0:T(8,128)(2,1)S(1)}, u32[]{:S(2)}, u32[]{:S(2)}) async-start(bf16[4,2048,128]{2,1,0:T(8,128)(2,1)} %broadcast_in_dim.6), calls=%async_computation | async-start | bytes 4194304 | tf_op jit(solution)/shard_map/all_to_all | solution.py:24
  7.9 0.0 copy-done.2
  7.9 26.3 %all-to-all-done = bf16[4,2048,128]{2,1,0:T(8,128)(2,1)S(1)} async-done(((bf16[4,2048,128]{2,1,0:T(8,128)(2,1)}), bf16[4,2048,128]{2,1,0:T(8,128)(2,1)S(1)}, u32[]{:S(2)}, u32[]{:S(2)}) %all-to-all-start) | async-done | bytes 2097184 | tf_op jit(solution)/shard_map/all_to_all | solution.py:24
  34.2 0.0 copy-start.1
  34.2 1.7 %broadcast_in_dim.8 = bf16[32,64,512]{2,1,0:T(8,128)(2,1)} broadcast(bf16[64,512]{1,0:T(8,128)(2,1)S(1)} %copy_bitcast_fusion.2), dimensions={1,2} | broadcast | bytes 2162688 | tf_op jit(solution)/shard_map/broadcast_in_dim | solution.py:25
  35.9 0.3 copy-done.1
  36.2 8.5 %all-to-all-start.1 = ((bf16[32,64,512]{2,1,0:T(8,128)(2,1)}), bf16[32,64,512]{2,1,0:T(8,128)(2,1)}, u32[]{:S(2)}, u32[]{:S(2)}) async-start(bf16[32,64,512]{2,1,0:T(8,128)(2,1)} %broadcast_in_dim.8), calls=%async_computation.1 | async-start | bytes 4194304 | tf_op jit(solution)/shard_map/all_to_all | solution.py:24
  44.7 1.8 %copy_bitcast_fusion = bf16[2048,512]{1,0:T(8,128)(2,1)S(1)} fusion(bf16[4,2048,128]{2,1,0:T(8,128)(2,1)} %copy-done.1), kind=kLoop, calls=%fused_computation.4 | loop fusion | bytes 4194304 | tf_op jit(solution)/shard_map/reshape | solution.py:19
  46.5 5.1 %gather_fusion = bf16[1024,512]{1,0:T(8,128)(2,1)} fusion(bf16[2048,512]{1,0:T(8,128)(2,1)S(1)} %copy_bitcast_fusion, s32[1024]{0:T(1024)S(1)} %broadcast_clamp_fusion.1), kind=kCustom, calls=%fused_computation | custom fusion | bytes 2101248 | tf_op jit(solution)/shard_map/gather | solution.py:217
  51.6 0.0 copy-start.3
  51.6 0.2 collective-permute-start
  51.8 5.1 %gather_fusion.1 = bf16[1024,512]{1,0:T(8,128)(2,1)} fusion(bf16[2048,512]{1,0:T(8,128)(2,1)S(1)} %copy_bitcast_fusion, s32[1024]{0:T(1024)S(1)} %broadcast_clamp_fusion), kind=kCustom, calls=%fused_computation.1 | custom fusion | bytes 2101248 | tf_op jit(solution)/shard_map/gather | solution.py:217
  56.9 4.9 %collective-permute-start.1 = (bf16[1024,512]{1,0:T(8,128)(2,1)}, bf16[1024,512]{1,0:T(8,128)(2,1)}, u32[]{:S(2)}, u32[]{:S(2)}) collective-permute-start(bf16[1024,512]{1,0:T(8,128)(2,1)} %gather_fusion.1), channel_id=1, source_target_pairs={{4,0},{8,4},{12,8},{16,12},{20,16},{24,20},{28,24},{32,28},{36,32}... | collective-permute-start | bytes 3145736 | tf_op jit(solution)/shard_map/ppermute | solution.py:42
  61.8 0.1 add.102
  61.8 0.1 add.103
  61.9 0.0 copy-done.3
  61.9 0.1 copy.32
  62.0 0.1 squeeze.11
  62.8 11.0 %all-to-all-done.1 = bf16[32,64,512]{2,1,0:T(8,128)(2,1)} async-done(((bf16[32,64,512]{2,1,0:T(8,128)(2,1)}), bf16[32,64,512]{2,1,0:T(8,128)(2,1)}, u32[]{:S(2)}, u32[]{:S(2)}) %all-to-all-start.1) | async-done | bytes 2097184 | tf_op jit(solution)/shard_map/all_to_all | solution.py:24
  73.8 3.1 %gather_fusion.2 = bf16[256,512]{1,0:T(8,128)(2,1)S(1)} fusion(bf16[2048,512]{1,0:T(8,128)(2,1)} %bitcast.5, s32[1024]{0:T(1024)S(1)} %pad_clamp_fusion), kind=kCustom, calls=%fused_computation.2 | custom fusion | bytes 525312 | tf_op jit(solution)/shard_map/gather | solution.py:221
  76.9 8.0 %collective-permute-done = bf16[1024,512]{1,0:T(8,128)(2,1)} collective-permute-done((bf16[1024,512]{1,0:T(8,128)(2,1)}, bf16[1024,512]{1,0:T(8,128)(2,1)}, u32[]{:S(2)}, u32[]{:S(2)}) %collective-permute-start) | collective-permute-done | bytes 1048608 | tf_op jit(solution)/shard_map/ppermute | solution.py:39
  84.8 0.0 collective-permute-done.1
  84.8 3.5 %pad_maximum_fusion.table_ref = bf16[4352,512]{1,0:T(8,128)(2,1)} fusion(bf16[256,512]{1,0:T(8,128)(2,1)S(1)} %gather_fusion.2, bf16[1024,512]{1,0:T(8,128)(2,1)} %collective-permute-done.1, bf16[1024,512]{1,0:T(8,128)(2,1)} %collective-permute-done, bf16[2048,512]{1,0:T(8,128)(2,1)S(1)} %copy_bitcast_fusion), kind=kLoop, calls=%fused_computation.3 | loop fusion | flops 17825792 | bytes 8912896 | tf_op jit(solution)/shard_map/concatenate | solution.py:222
  88.3 31.9 %shard_map.194 = (bf16[2048,512]{1,0:T(8,128)(2,1)}, bf16[2048,512]{1,0:T(8,128)(2,1)}) custom-call(s32[1]{0:T(128)S(6)} %copy.43.count_ref, bf16[4352,512]{1,0:T(8,128)(2,1)} %pad_maximum_fusion.table_ref, bf16[2048,512]{1,0:T(8,128)(2,1)} %edges_ref.1, s32[16,128]{1,0:T(8,128)} %bitcast.41, s32[16,128]{1,0:T(8,128)} %bitcast.42, ...), custom_call_target="tpu_custom_call" | custom-call | tf_op jit(solution)/shard_map/pallas_call | solution.py:160
  120.2 4.5 %all-to-all-start.2 = ((bf16[4,512,512]{2,1,0:T(8,128)(2,1)}), bf16[4,512,512]{2,1,0:T(8,128)(2,1)}, u32[]{:S(2)}, u32[]{:S(2)}) async-start(bf16[4,512,512]{2,1,0:T(8,128)(2,1)} %bitcast.37), calls=%async_computation.2 | async-start | bytes 4194304 | tf_op jit(solution)/shard_map/all_to_all | solution.py:55
  124.6 0.0 copy-start.6
  124.6 0.0 copy-start.7
  124.7 2.5 %fusion.6 = f32[512,512]{1,0:T(8,128)} fusion(bf16[1024,512]{1,0:T(8,128)(2,1)} %param.32, bf16[2048,512]{1,0:T(8,128)(2,1)S(1)} %copy_bitcast_fusion, s32[]{:T(128)S(6)} %select_n.33), kind=kOutput, calls=%fused_computation.16 | convolution fusion | flops 268435456 | bytes 2097156 | tf_op jit(solution)/shard_map/dot_general | solution.py:244
  127.1 21.0 %all-to-all-done.2 = bf16[4,512,512]{2,1,0:T(8,128)(2,1)} async-done(((bf16[4,512,512]{2,1,0:T(8,128)(2,1)}), bf16[4,512,512]{2,1,0:T(8,128)(2,1)}, u32[]{:S(2)}, u32[]{:S(2)}) %all-to-all-start.2) | async-done | bytes 2097184 | tf_op jit(solution)/shard_map/all_to_all | solution.py:55
  148.1 2.2 %reduce_sum.30 = bf16[512,512]{1,0:T(8,128)(2,1)S(1)} reduce(bf16[4,512,512]{2,1,0:T(8,128)(2,1)} %all-to-all-done.2, bf16[]{:T(256)} %constant.6.clone.1), dimensions={0}, to_apply=%region_0.0 | reduce | flops 786432 | bytes 2621442 | tf_op jit(solution)/shard_map/reduce_sum | solution.py:56
  150.3 0.0 copy-done
  150.3 0.0 copy-done.6
  150.3 0.0 copy-done.7
  150.3 0.0 copy-start.4
  150.3 0.0 copy-start.5
  150.3 3.2 %fusion.11 = (f32[512]{0:T(512)S(1)}, f32[512,512]{1,0:T(8,128)}) fusion(f32[512]{0:T(512)S(1)} %copy-done.6, bf16[512,512]{1,0:T(8,128)(2,1)S(1)} %copy-done, f32[512,512]{1,0:T(8,128)} %fusion.6, bf16[512,512]{1,0:T(8,128)(2,1)S(1)} %reduce_sum.30, f32[512]{0:T(512)S(1)} %copy-done.7, bf16[1024,512]{1,0:T(8,128)(2,1)} %param.32), kind=kOutput, calls=%fused_computation.32 | convolution fusion | flops 539229696 | bytes 3676160 | tf_op jit(solution)/shard_map/dot_general | solution.py:253
  153.6 1.5 multiply_reduce_fusion
  155.1 0.0 copy-done.4
  155.1 0.0 copy-done.5
  155.1 1.5 copy_bitcast_fusion.1
  156.6 10.5 %all_to_all.34 = bf16[512,4,128]{2,0,1:T(8,128)(2,1)S(1)} all-to-all(bf16[512,4,128]{2,0,1:T(8,128)(2,1)S(1)} %copy_bitcast_fusion.1), channel_id=1, replica_groups=mesh['patch'=32,'hidden'=4] {'hidden'}, dimensions={1} | all-to-all | bytes 1048576 | tf_op jit(solution)/shard_map/all_to_all | solution.py:256
  167.1 0.8 copy.44
  (9 shorter events, 0.1 us)
Async XLA Ops:
  0.6 149.7 %copy-start = (bf16[512,512]{1,0:T(8,128)(2,1)S(1)}, bf16[512,512]{1,0:T(8,128)(2,1)}, u32[]{:S(2)}) copy-start(bf16[512,512]{1,0:T(8,128)(2,1)} %param.34) | copy-start | bytes 1572868
  3.3 4.5 %copy-start.2 = (s32[1,2,1024]{2,1,0:T(2,128)S(1)}, s32[1,2,1024]{2,1,0:T(2,128)}, u32[]{:S(2)}) copy-start(s32[1,2,1024]{2,1,0:T(2,128)} %param.23) | copy-start | bytes 24580
  3.3 30.9 %all-to-all-start = ((bf16[4,2048,128]{2,1,0:T(8,128)(2,1)}), bf16[4,2048,128]{2,1,0:T(8,128)(2,1)S(1)}, u32[]{:S(2)}, u32[]{:S(2)}) async-start(bf16[4,2048,128]{2,1,0:T(8,128)(2,1)} %broadcast_in_dim.6), calls=%async_computation | async-start | bytes 4194304 | tf_op jit(solution)/shard_map/all_to_all | solution.py:24
  34.2 2.0 %copy-start.1 = (bf16[4,2048,128]{2,1,0:T(8,128)(2,1)}, bf16[4,2048,128]{2,1,0:T(8,128)(2,1)S(1)}, u32[]{:S(2)}) copy-start(bf16[4,2048,128]{2,1,0:T(8,128)(2,1)S(1)} %all-to-all-done) | copy-start | bytes 6291460
  36.2 37.6 %all-to-all-start.1 = ((bf16[32,64,512]{2,1,0:T(8,128)(2,1)}), bf16[32,64,512]{2,1,0:T(8,128)(2,1)}, u32[]{:S(2)}, u32[]{:S(2)}) async-start(bf16[32,64,512]{2,1,0:T(8,128)(2,1)} %broadcast_in_dim.8), calls=%async_computation.1 | async-start | bytes 4194304 | tf_op jit(solution)/shard_map/all_to_all | solution.py:24
  51.6 10.3 %copy-start.3 = (s32[1,32,8]{1,2,0:T(8,128)S(1)}, s32[1,32,8]{1,2,0:T(8,128)}, u32[]{:S(2)}) copy-start(s32[1,32,8]{1,2,0:T(8,128)} %param.24) | copy-start | bytes 3076
  51.6 33.2 %collective-permute-start = (bf16[1024,512]{1,0:T(8,128)(2,1)}, bf16[1024,512]{1,0:T(8,128)(2,1)}, u32[]{:S(2)}, u32[]{:S(2)}) collective-permute-start(bf16[1024,512]{1,0:T(8,128)(2,1)} %gather_fusion), channel_id=1, source_target_pairs={{0,4},{4,8},{8,12},{12,16},{16,20},{20,24},{24,28},{28,32},{32,36}... | collective-permute-start | bytes 3145736 | tf_op jit(solution)/shard_map/ppermute | solution.py:39
  56.9 27.9 %collective-permute-start.1 = (bf16[1024,512]{1,0:T(8,128)(2,1)}, bf16[1024,512]{1,0:T(8,128)(2,1)}, u32[]{:S(2)}, u32[]{:S(2)}) collective-permute-start(bf16[1024,512]{1,0:T(8,128)(2,1)} %gather_fusion.1), channel_id=1, source_target_pairs={{4,0},{8,4},{12,8},{16,12},{20,16},{24,20},{28,24},{32,28},{36,32}... | collective-permute-start | bytes 3145736 | tf_op jit(solution)/shard_map/ppermute | solution.py:42
  120.2 27.9 %all-to-all-start.2 = ((bf16[4,512,512]{2,1,0:T(8,128)(2,1)}), bf16[4,512,512]{2,1,0:T(8,128)(2,1)}, u32[]{:S(2)}, u32[]{:S(2)}) async-start(bf16[4,512,512]{2,1,0:T(8,128)(2,1)} %bitcast.37), calls=%async_computation.2 | async-start | bytes 4194304 | tf_op jit(solution)/shard_map/all_to_all | solution.py:55
  124.6 25.7 %copy-start.6 = (f32[512]{0:T(512)S(1)}, f32[512]{0:T(512)}, u32[]{:S(2)}) copy-start(f32[512]{0:T(512)} %param.35) | copy-start | bytes 6148
  124.6 25.7 %copy-start.7 = (f32[512]{0:T(512)S(1)}, f32[512]{0:T(512)}, u32[]{:S(2)}) copy-start(f32[512]{0:T(512)} %param.33) | copy-start | bytes 6148
  150.3 4.8 %copy-start.4 = (f32[512]{0:T(512)S(1)}, f32[512]{0:T(512)}, u32[]{:S(2)}) copy-start(f32[512]{0:T(512)} %param.37) | copy-start | bytes 6148
  150.3 4.8 %copy-start.5 = (f32[512]{0:T(512)S(1)}, f32[512]{0:T(512)}, u32[]{:S(2)}) copy-start(f32[512]{0:T(512)} %param.36) | copy-start | bytes 6148

commit v2 on v1

v2 whole, which is shorter than its diff:
```python
import jax
import jax.numpy as jnp
from jax import lax
from jax.experimental import pallas as pl
from jax.experimental.pallas import tpu as pltpu
from jax.sharding import PartitionSpec as P

COARSE_DEV = 64
LANES = 128
ROW_BLOCK = 512
CHUNKS = 4
MESH = pl.DeviceIdType.MESH


layer_epsilon = 1e-05

TO_RIGHT, TO_LEFT, RELAY_RIGHT, RELAY_LEFT = 0, 4, 8, 10
FORWARD, BACKWARD, COARSE, PICKED = 12, 16, 20, 21
SLOTS = 24
L_NODES, L_EDGES, L_IN, L_OUT, L_RESULT = 0, 1, 2, 3, 4
LOCALS = 12


def in_blocks(array, dim, count):
    lengths = array.shape
    blocks = array.reshape(*lengths[:dim], count, lengths[dim] // count, *lengths[dim + 1 :])
    return jnp.moveaxis(blocks, dim, 0)


def sent_and_summed(array, axis, dim):
    blocks = in_blocks(array, dim, lax.axis_size(axis))
    arrived = lax.all_to_all(blocks, axis, split_axis=0, concat_axis=0, tiled=True)
    return arrived.astype(jnp.float32).sum(axis=0)


def normalize(output, norm_gain, norm_shift):
    row_mean = jnp.mean(output, axis=1, keepdims=True)
    centered = output - row_mean
    row_var = jnp.mean(jnp.square(centered), axis=1, keepdims=True)
    return centered * lax.rsqrt(row_var + layer_epsilon) * norm_gain + norm_shift


def silu(v):
    half = 0.5 * v
    return half + half * jnp.tanh(half)


def one_hot_rows(ids_ref, out_ref, offset=None):
    rows, width = out_ref.shape
    lane = lax.broadcasted_iota(jnp.int32, (LANES, LANES), 1)

    def block(r, carry):
        line = ids_ref[pl.ds(r, 1), :]
        if offset is not None:
            line = line + offset(r)
        ids = jnp.broadcast_to(line, (LANES, LANES)).T
        here = pl.ds(pl.multiple_of(r * LANES, LANES), LANES)
        for k in range(width // LANES):
            out_ref[here, k * LANES : (k + 1) * LANES] = jnp.where(
                ids == lane + k * LANES, 1.0, 0.0
            ).astype(jnp.bfloat16)
        return carry

    lax.fori_loop(0, rows // LANES, block, 0)


def layer_kernel(
    coarse_dev,
    count_ref,
    nodes_ref,
    edges_ref,
    senders_ref,
    receivers_ref,
    halo_ref,
    coarse_ref,
    w_in_ref,
    b_in_ref,
    w_out_ref,
    b_out_ref,
    gain_ref,
    shift_ref,
    edges_out_ref,
    sums_ref,
    own_rows_ref,
    table,
    outgoing,
    everyone,
    hot_halo,
    hot_send,
    hot_recv,
    hot_pick,
    send_rows,
    recv_rows,
    pre,
    edges,
    sent,
    w_in,
    w_out,
    send_sem,
    recv_sem,
    local_sem,
):
    p, h = lax.axis_index("patch"), lax.axis_index("hidden")
    patches, shards = lax.axis_size("patch"), lax.axis_size("hidden")
    right, left, far = (lax.rem(h + s, shards) for s in (1, shards - 1, 2))
    after, before = lax.rem(p + 1, patches), lax.rem(p + patches - 1, patches)
    node_rows = nodes_ref.shape[0]
    edge_rows, columns = edges_ref.shape
    border = outgoing.shape[1] // 2
    chunk = node_rows // CHUNKS
    block = min(ROW_BLOCK, edge_rows)

    def copy_to(source, target, slot, q, g):
        return pltpu.make_async_remote_copy(
            src_ref=source,
            dst_ref=target,
            send_sem=send_sem.at[slot],
            recv_sem=recv_sem.at[slot],
            device_id={"patch": q, "hidden": g},
            device_id_type=MESH,
        )

    def rows_of(part, k):
        return table.at[part, pl.ds(k * chunk, chunk), :]

    barrier = pltpu.get_barrier_semaphore()

    def greet(j, carry):
        pl.semaphore_signal(
            barrier,
            inc=1,
            device_id={"patch": lax.rem(p + j, patches), "hidden": h},
            device_id_type=MESH,
        )
        return carry

    for g in (right, left, far):
        pl.semaphore_signal(barrier, inc=1, device_id={"patch": p, "hidden": g}, device_id_type=MESH)
    lax.fori_loop(1, patches, greet, 0)

    nodes_in = pltpu.make_async_copy(
        nodes_ref, table.at[h, pl.ds(0, node_rows), :], local_sem.at[L_NODES]
    )
    edges_in = pltpu.make_async_copy(edges_ref, edges, local_sem.at[L_EDGES])
    w_in_in = pltpu.make_async_copy(w_in_ref, w_in, local_sem.at[L_IN])
    w_out_in = pltpu.make_async_copy(w_out_ref, w_out, local_sem.at[L_OUT])
    for c in (nodes_in, edges_in, w_in_in, w_out_in):
        c.start()

    one_hot_rows(halo_ref, hot_halo)
    pl.semaphore_wait(barrier, patches + 2)
    nodes_in.wait()

    to_right = [copy_to(rows_of(h, k), rows_of(h, k), TO_RIGHT + k, p, right) for k in range(CHUNKS)]
    to_left = [copy_to(rows_of(h, k), rows_of(h, k), TO_LEFT + k, p, left) for k in range(CHUNKS)]
    for a, b in ((0, 2), (1, 3), (2, 0), (3, 1)):
        to_right[a].start()
        to_left[b].start()

    slot_rows = pl.ds(pl.multiple_of(p * coarse_dev, coarse_dev), coarse_dev)
    own_coarse = table.at[h, pl.ds(0, coarse_dev), :]

    def share(j, carry):
        copy_to(own_coarse, everyone.at[slot_rows, :], COARSE, lax.rem(p + j, patches), h).start()
        return carry

    lax.fori_loop(1, patches, share, 0)
    everyone[slot_rows, :] = own_coarse[...]

    border_blocks = 2 * border // min(ROW_BLOCK, 2 * border)

    def send_halo(parts, names):
        width = len(parts) * LANES
        source = jnp.concatenate([table[c, :node_rows, :] for c in parts], axis=1)
        size = 2 * border // border_blocks

        def piece(i, carry):
            here = pl.ds(pl.multiple_of(i * size, size), size)
            result = jnp.dot(
                hot_halo[here, :],
                jnp.concatenate([table[c, :node_rows, :] for c in parts], axis=1),
                preferred_element_type=jnp.float32,
            ).astype(jnp.bfloat16)
            for n, name in enumerate(names):
                outgoing[name, here, :] = result[:, n * LANES : (n + 1) * LANES]
            return carry

        lax.fori_loop(0, border_blocks, piece, 0)
        copies = []
        for part, name in zip(parts, names):
            back = copy_to(
                outgoing.at[name, pl.ds(0, border), :],
                table.at[part, pl.ds(node_rows + border, border), :],
                BACKWARD + name,
                before,
                h,
            )
            forth = copy_to(
                outgoing.at[name, pl.ds(border, border), :],
                table.at[part, pl.ds(node_rows, border), :],
                FORWARD + name,
                after,
                h,
            )
            back.start()
            forth.start()
            copies += [back, forth]
        return copies

    halos = {}
    halos[0] = send_halo((h,), (0,))

    edges_in.wait()
    w_in_in.wait()

    def self_block(i, carry):
        here = pl.ds(pl.multiple_of(i * block, block), block)
        pre[here, :] = (
            jnp.dot(edges[here, :], w_in[:columns, :], preferred_element_type=jnp.float32)
            + b_in_ref[...]
        )
        return carry

    lax.fori_loop(0, edge_rows // block, self_block, 0)

    one_hot_rows(receivers_ref, hot_recv)
    per_slot = hot_pick.shape[0] // patches
    spot = lax.broadcasted_iota(jnp.int32, (1, LANES), 1)
    one_hot_rows(
        coarse_ref, hot_pick, lambda r: lax.div(r * LANES + spot, per_slot) * coarse_dev
    )

    def from_left(k):
        return copy_to(rows_of(left, k), rows_of(left, k), TO_RIGHT + k, p, right)

    def from_right(k):
        return copy_to(rows_of(right, k), rows_of(right, k), TO_LEFT + k, p, left)

    relay_right = [copy_to(rows_of(left, k), rows_of(left, k), RELAY_RIGHT + k, p, right) for k in (0, 1)]
    relay_left = [copy_to(rows_of(right, k + 2), rows_of(right, k + 2), RELAY_LEFT + k, p, left) for k in (0, 1)]
    for k in (0, 1):
        from_left(k).wait_recv()
        relay_right[k].start()
        from_right(k + 2).wait_recv()
        relay_left[k].start()

    peers = (patches - 1) * coarse_dev
    all_coarse = copy_to(
        everyone.at[pl.ds(0, peers), :], everyone.at[pl.ds(0, peers), :], COARSE, after, h
    )
    all_coarse.wait_recv()
    first_picked = node_rows + 2 * border
    picked_rows = hot_pick.shape[0]
    picked = table.at[h, pl.ds(first_picked, picked_rows), :]
    table[h, first_picked : first_picked + picked_rows, :] = jnp.dot(
        hot_pick[...], everyone[...], preferred_element_type=jnp.float32
    ).astype(jnp.bfloat16)
    pick_copies = [copy_to(picked, picked, PICKED + n, p, g) for n, g in enumerate((right, left, far))]
    for c in pick_copies:
        c.start()

    one_hot_rows(senders_ref, hot_send)

    for k in (2, 3):
        from_left(k).wait_recv()
        from_right(k - 2).wait_recv()
    halos[1] = send_halo((left, right), (1, 2))

    def gather(hot, low, high, parts, into, add):
        def piece(i, carry):
            here = pl.ds(pl.multiple_of(i * block, block), block)
            result = jnp.dot(
                hot[here, low:high],
                jnp.concatenate([table[c, low:high, :] for c in parts], axis=1),
                preferred_element_type=jnp.float32,
            ).astype(jnp.bfloat16)
            for n, c in enumerate(parts):
                value = result[:, n * LANES : (n + 1) * LANES]
                into[c, here, :] = into[c, here, :] + value if add else value
            return carry

        lax.fori_loop(0, edge_rows // block, piece, 0)

    gather(hot_recv, 0, node_rows, (left, right), recv_rows, False)
    gather(hot_send, 0, node_rows, (left, right), send_rows, False)

    for k in (0, 1):
        copy_to(rows_of(far, k), rows_of(far, k), RELAY_RIGHT + k, p, right).wait_recv()
        copy_to(rows_of(far, k + 2), rows_of(far, k + 2), RELAY_LEFT + k, p, left).wait_recv()
    halos[2] = send_halo((far,), (3,))

    gather(hot_recv, 0, node_rows, (h, far), recv_rows, False)
    gather(hot_send, 0, node_rows, (h, far), send_rows, False)
    total_rows = table.shape[1]
    for c in halos[1]:
        c.wait_recv()
    for n, g in enumerate((left, right, far)):
        landed = table.at[g, pl.ds(first_picked, picked_rows), :]
        copy_to(landed, landed, PICKED + n, p, right).wait_recv()
    gather(hot_send, node_rows, total_rows, (left, right), send_rows, True)
    for c in halos[0] + halos[2]:
        c.wait_recv()
    gather(hot_send, node_rows, total_rows, (h, far), send_rows, True)

    w_out_in.wait()

    def edge_block(i, carry):
        start = pl.multiple_of(i * block, block)
        here = pl.ds(start, block)
        gathered = jnp.concatenate(
            [send_rows[c, here, :] for c in range(columns // LANES)]
            + [recv_rows[c, here, :] for c in range(columns // LANES)],
            axis=1,
        )
        value = pre[here, :] + jnp.dot(
            gathered, w_in[columns:, :], preferred_element_type=jnp.float32
        )
        active = silu(value).astype(jnp.bfloat16)
        output = jnp.dot(active, w_out[...], preferred_element_type=jnp.float32) + b_out_ref[...]
        update = normalize(output, gain_ref[...], shift_ref[...])
        position = start + lax.broadcasted_iota(jnp.int32, (block, 1), 0)
        message = jnp.where(position < count_ref[0], update, 0.0)
        sent[here, :] = message.astype(jnp.bfloat16)
        edges[here, :] = (edges[here, :].astype(jnp.float32) + message).astype(jnp.bfloat16)
        return carry

    lax.fori_loop(0, edge_rows // block, edge_block, 0)
    edges_done = pltpu.make_async_copy(edges, edges_out_ref, local_sem.at[L_RESULT])
    edges_done.start()

    share_rows = node_rows // shards

    def sum_block(j, carry):
        start = pl.multiple_of(j * share_rows, share_rows)
        node = start + lax.broadcasted_iota(jnp.int32, (share_rows, LANES), 0)
        for k in range(edge_rows // LANES):
            ids = jnp.broadcast_to(receivers_ref[k : k + 1, :], (share_rows, LANES))
            hot_recv[:share_rows, k * LANES : (k + 1) * LANES] = jnp.where(
                node == ids, 1.0, 0.0
            ).astype(jnp.bfloat16)
        sums_ref[pl.ds(start, share_rows), :] = jnp.dot(
            hot_recv[:share_rows, :edge_rows], sent[...], preferred_element_type=jnp.float32
        ).astype(jnp.bfloat16)
        return carry

    lax.fori_loop(0, shards, sum_block, 0)
    mine = pl.ds(pl.multiple_of(h * share_rows, share_rows), share_rows)
    for c in range(columns // LANES):
        own_rows_ref[:, c * LANES : (c + 1) * LANES] = table[c, mine, :]

    for c in to_right + to_left + relay_right + relay_left + pick_copies:
        c.wait_send()
    for c in halos[0] + halos[1] + halos[2]:
        c.wait_send()
    all_coarse.wait_send()
    edges_done.wait()


def layer_stage(nodes, edges, senders, receivers, halo_rows, coarse_rows, edge_count, w_in, b_in, w_out, b_out, gain, shift):
    edge_rows, columns = edges.shape
    node_rows = nodes.shape[0]
    border = halo_rows.shape[2]
    picked = coarse_rows.shape[1] * coarse_rows.shape[2]
    total = node_rows + 2 * border + picked
    shards = lax.axis_size("hidden")
    patches = lax.axis_size("patch")
    vmem = pl.BlockSpec(memory_space=pltpu.VMEM)
    smem = pl.BlockSpec(memory_space=pltpu.SMEM)
    far_away = pl.BlockSpec(memory_space=pl.ANY)
    bf16 = jnp.bfloat16
    parts = columns // LANES
    return pl.pallas_call(
        lambda *refs: layer_kernel(COARSE_DEV, *refs),
        out_shape=(
            jax.ShapeDtypeStruct((edge_rows, columns), bf16),
            jax.ShapeDtypeStruct((node_rows, columns), bf16),
            jax.ShapeDtypeStruct((node_rows // shards, columns), bf16),
        ),
        in_specs=[smem, far_away, far_away, vmem, vmem, vmem, vmem, far_away, vmem, far_away, vmem, vmem, vmem],
        out_specs=(far_away, vmem, vmem),
        scratch_shapes=[
            pltpu.VMEM((parts, total, LANES), bf16),
            pltpu.VMEM((parts, 2 * border, LANES), bf16),
            pltpu.VMEM((patches * COARSE_DEV, LANES), bf16),
            pltpu.VMEM((2 * border, node_rows), bf16),
            pltpu.VMEM((edge_rows, total), bf16),
            pltpu.VMEM((edge_rows, node_rows), bf16),
            pltpu.VMEM((picked, patches * COARSE_DEV), bf16),
            pltpu.VMEM((parts, edge_rows, LANES), bf16),
            pltpu.VMEM((parts, edge_rows, LANES), bf16),
            pltpu.VMEM((edge_rows, columns), jnp.float32),
            pltpu.VMEM((edge_rows, columns), bf16),
            pltpu.VMEM((edge_rows, columns), bf16),
            pltpu.VMEM(w_in.shape, bf16),
            pltpu.VMEM(w_out.shape, bf16),
            pltpu.SemaphoreType.DMA((SLOTS,)),
            pltpu.SemaphoreType.DMA((SLOTS,)),
            pltpu.SemaphoreType.DMA((LOCALS,)),
        ],
        compiler_params=pltpu.CompilerParams(
            vmem_limit_bytes=67043328, collective_id=0, has_side_effects=True
        ),
    )(
        edge_count,
        nodes,
        edges,
        senders.reshape(-1, LANES),
        receivers.reshape(-1, LANES),
        halo_rows.reshape(-1, LANES),
        coarse_rows.reshape(-1, LANES),
        w_in,
        b_in.reshape(1, -1),
        w_out,
        b_out.reshape(1, -1),
        gain.reshape(1, -1),
        shift.reshape(1, -1),
    )


def local(
    nodes,
    edges,
    senders,
    receivers,
    halo_rows,
    coarse_rows,
    edge_count,
    w_edge_in,
    b_edge_in,
    w_edge_out,
    b_edge_out,
    edge_gain,
    edge_shift,
    w_node_in,
    b_node_in,
    w_node_out,
    b_node_out,
    node_gain,
    node_shift,
):
    columns = edges.shape[1]
    edges_out, summed, own_rows = layer_stage(
        nodes,
        edges,
        senders,
        receivers,
        halo_rows,
        coarse_rows,
        edge_count,
        w_edge_in,
        b_edge_in,
        w_edge_out,
        b_edge_out,
        edge_gain,
        edge_shift,
    )
    aggregated = sent_and_summed(summed, "hidden", 0)
    pre_active = jnp.dot(own_rows, w_node_in[:columns], preferred_element_type=jnp.float32)
    pre_active = (
        pre_active
        + jnp.dot(
            aggregated.astype(jnp.bfloat16), w_node_in[columns:], preferred_element_type=jnp.float32
        )
        + b_node_in
    )
    active = jax.nn.silu(pre_active).astype(jnp.bfloat16)
    output = jnp.dot(active, w_node_out, preferred_element_type=jnp.float32) + b_node_out
    update = normalize(output, node_gain, node_shift)
    new_rows = (own_rows.astype(jnp.float32) + update).astype(jnp.bfloat16)
    nodes_out = lax.all_to_all(new_rows, "hidden", split_axis=1, concat_axis=0, tiled=True)
    return (nodes_out, edges_out)


def solution(mesh):
    return jax.shard_map(
        local,
        mesh=mesh,
        in_specs=(
            P("patch", "hidden"),
            P(("patch", "hidden"), None),
            P(("patch", "hidden")),
            P(("patch", "hidden")),
            P("patch", None, None),
            P("patch", None, None),
            P(("patch", "hidden")),
            *([P()] * 12),
        ),
        out_specs=(P("patch", "hidden"), P(("patch", "hidden"), None)),
        check_vma=False,
    )
```

time: 170 us -> 115 us (0.68)
  waiting for transfers between devices: 66.2 us -> 31.3 us
  Pallas kernels: 31.9 us -> 60 us
  local copies, waits for them, and re-layouts: 20.9 us -> 4.86 us
  starting transfers between devices: 22.5 us -> 7.22 us
  blocking collectives: 10.5 us -> 0 us
  other arithmetic: 8.74 us -> 3.82 us
    all_to_all x2 -> x1, waiting for transfers between devices: 37.3 us -> 8.05 us  [local(): lax.all_to_all(new_rows, 'hidden', split_axis=1, concat_axis=0, tiled=True)]
    pallas_call x1, Pallas kernels: 31.9 us -> 60 us  [layer_stage(): pl.pallas_call(lambda *refs: layer_kernel(COARSE_DEV, *refs), out_shape=(...]
    gather x3 -> x0, local copies, waits for them, and re-layouts: 13.2 us -> none  [the longest x1 5.08 us: local(): own_block[halo_rows[0, 1]]]
    all_to_all x1 -> x0, blocking collectives: 10.5 us -> none  [local(): lax.all_to_all(new_rows, 'hidden', split_axis=1, concat_axis=0, tiled=True)]
    all_to_all x2 -> x1, starting transfers between devices: 13 us -> 3.47 us  [local(): lax.all_to_all(new_rows, 'hidden', split_axis=1, concat_axis=0, tiled=True)]
    ppermute x2 -> x0, waiting for transfers between devices: 7.97 us -> none  [the longest x1 7.97 us: extended(): lax.ppermute(lax.slice_in_dim(block, block.shape[dim] - width, None, axis...]
    ppermute x2 -> x0, starting transfers between devices: 5.07 us -> none  [the longest x1 4.87 us: extended(): lax.ppermute(lax.slice_in_dim(block, 0, width, axis=dim), axis, backward)]
    broadcast_in_dim x3 -> x0, local copies, waits for them, and re-layouts: 4.43 us -> none  [from_everyone(): jnp.broadcast_to(array[None], (count, *array.shape))]
  transfers between devices with their start and end apart: 5 -> 2, of which waited for: 4 -> 2; matrix products, arithmetic and copies ran while one was open for 11% -> 2% of each run, Pallas kernels for 0% -> 0%
where the time goes in v2:
time: 115 us; the launch traced here: 114 us
  Pallas kernels  60 us (52%)
  waiting for transfers between devices  31.3 us (27%)
  starting transfers between devices  7.22 us (6%)
  matrix products  5.1 us (4%)
  local copies, waits for them, and re-layouts  4.86 us (4%)
  other arithmetic  3.82 us (3%)
  between operations  1.37 us (1%)
    pallas_call x1, Pallas kernels, layer_stage(): pl.pallas_call(lambda *refs: layer_kernel(COARSE_DEV, *refs), out_shape=(...  60 us
    all_to_all x1, waiting for transfers between devices, sent_and_summed(): lax.all_to_all(blocks, axis, split_axis=0, concat_axis=0, tiled=True)  23.2 us
    all_to_all x1, waiting for transfers between devices, local(): lax.all_to_all(new_rows, 'hidden', split_axis=1, concat_axis=0, tiled=True)  8.05 us
    all_to_all x1, starting transfers between devices, sent_and_summed(): lax.all_to_all(blocks, axis, split_axis=0, concat_axis=0, tiled=True)  3.75 us
    all_to_all x1, starting transfers between devices, local(): lax.all_to_all(new_rows, 'hidden', split_axis=1, concat_axis=0, tiled=True)  3.47 us
    unnamed x15, local copies, waits for them, and re-layouts  2.9 us
    dot_general x1, matrix products, local(): jnp.dot(active, w_node_out, preferred_element_type=jnp.float32) + b_node_out  2.65 us
    dot_general x1, matrix products, local(): jnp.dot(own_rows, w_node_in[:columns], preferred_element_type=jnp.float32)  2.46 us
  transfers between devices with their start and end apart: 2, of which 2 were waited for; matrix products, arithmetic and copies ran while one was open for 2% of the time, Pallas kernels for 0%

profile of v2, /device:TPU:0, one launch (start us, length us, event | category | flops | bytes accessed | tf_op | source)
XLA Modules:
  0.0 113.6 jit_solution(430763733288798772)
XLA Ops:
  1.3 1.3 %reshape.52.refs_5_ = s32[16,128]{1,0:T(8,128)} reshape(s32[1,2,1024]{2,1,0:T(2,128)} %param.23) | data formatting | bytes 16384 | tf_op jit(solution)/shard_map/reshape | solution.py:409
  2.6 0.8 copy.27
  3.3 0.7 reshape.53.refs_6_
  4.0 60.0 %shard_map.194 = (bf16[2048,512]{1,0:T(8,128)(2,1)}, bf16[2048,512]{1,0:T(8,128)(2,1)}, bf16[512,512]{1,0:T(8,128)(2,1)}) custom-call(s32[1]{0:T(128)S(6)} %copy.35.refs_0_, bf16[2048,128]{1,0:T(8,128)(2,1)} %refs_1_.1, bf16[2048,512]{1,0:T(8,128)(2,1)} %refs_2_.1, s32[16,128]{1,0:T(8,128)} %bitcast.20, s32[16,128]{1,0:T(8,128)} %bitcast.21, ...), custom_call_target="tpu_custom_call" | custom-call | tf_op jit(solution)/shard_map/pallas_call | solution.py:372
  64.0 0.0 copy-start.1
  64.0 3.8 %all-to-all-start = ((bf16[4,512,512]{2,1,0:T(8,128)(2,1)}), bf16[4,512,512]{2,1,0:T(8,128)(2,1)S(1)}, u32[]{:S(2)}, u32[]{:S(2)}) async-start(bf16[4,512,512]{2,1,0:T(8,128)(2,1)} %bitcast.18), calls=%async_computation | async-start | bytes 4194304 | tf_op jit(solution)/shard_map/all_to_all | solution.py:32
  67.7 0.0 copy-done.1
  67.8 0.0 copy-start.4
  67.8 0.0 copy-start.5
  67.8 2.5 %fusion.6 = f32[512,512]{1,0:T(8,128)} fusion(bf16[512,512]{1,0:T(8,128)(2,1)S(1)} %copy-done.1, bf16[1024,512]{1,0:T(8,128)(2,1)} %param.32), kind=kOutput, calls=%fused_computation.11 | convolution fusion | flops 268435456 | bytes 2097152 | tf_op jit(solution)/shard_map/dot_general | solution.py:458
  70.2 23.2 %all-to-all-done = bf16[4,512,512]{2,1,0:T(8,128)(2,1)S(1)} async-done(((bf16[4,512,512]{2,1,0:T(8,128)(2,1)}), bf16[4,512,512]{2,1,0:T(8,128)(2,1)S(1)}, u32[]{:S(2)}, u32[]{:S(2)}) %all-to-all-start) | async-done | bytes 2097184 | tf_op jit(solution)/shard_map/all_to_all | solution.py:32
  93.5 1.2 %reduce_sum.30 = bf16[512,512]{1,0:T(8,128)(2,1)} reduce(bf16[4,512,512]{2,1,0:T(8,128)(2,1)S(1)} %all-to-all-done, bf16[]{:T(256)} %constant.8.clone.1), dimensions={0}, to_apply=%region_0.0 | reduce | flops 786432 | bytes 2621442 | tf_op jit(solution)/shard_map/reduce_sum | solution.py:33
  94.7 0.0 copy-done.4
  94.7 0.0 copy-done.5
  94.7 0.0 copy-start.2
  94.7 0.0 copy-start.3
  94.7 2.6 %fusion.9 = (f32[512]{0:T(512)S(1)}, f32[512,512]{1,0:T(8,128)S(1)}) fusion(f32[512]{0:T(512)S(1)} %copy-done.4, bf16[512,512]{1,0:T(8,128)(2,1)} %param.34, f32[512,512]{1,0:T(8,128)} %fusion.6, bf16[512,512]{1,0:T(8,128)(2,1)} %reduce_sum.30, f32[512]{0:T(512)S(1)} %copy-done.5, bf16[1024,512]{1,0:T(8,128)(2,1)} %param.32), kind=kOutput, calls=%fused_computation.16 | convolution fusion | flops 539229696 | bytes 3676160 | tf_op jit(solution)/shard_map/dot_general | solution.py:467
  97.4 0.3 multiply_reduce_fusion
  97.7 0.0 copy-done.2
  97.7 0.0 copy-done.3
  97.7 0.0 copy-start
  97.7 2.3 %copy_bitcast_fusion = bf16[512,4,128]{2,0,1:T(8,128)(2,1)} fusion(f32[512,512]{1,0:T(8,128)S(1)} %get-tuple-element.9, bf16[512,512]{1,0:T(8,128)(2,1)} %get-tuple-element.5, f32[512]{0:T(512)S(1)} %copy-done.2, f32[512]{0:T(512)S(1)} %copy-done.3, f32[512]{0:T(512)S(1)} %add_rsqrt_fusion, f32[512]{0:T(512)S(1)} %broadcast_multiply_fusion), kind=kLoop, calls=%fused_computation.7 | loop fusion | flops 1835008 | bytes 2105344 | tf_op jit(solution)/shard_map/all_to_all | solution.py:470
  100.0 3.5 %all-to-all-start.1 = ((bf16[512,4,128]{2,0,1:T(8,128)(2,1)}), bf16[512,4,128]{2,0,1:T(8,128)(2,1)S(1)}, u32[]{:S(2)}, u32[]{:S(2)}) async-start(bf16[512,4,128]{2,0,1:T(8,128)(2,1)} %copy_bitcast_fusion), calls=%async_computation.1 | async-start | bytes 1048576 | tf_op jit(solution)/shard_map/all_to_all | solution.py:470
  103.5 8.0 %all-to-all-done.1 = bf16[512,4,128]{2,0,1:T(8,128)(2,1)S(1)} async-done(((bf16[512,4,128]{2,0,1:T(8,128)(2,1)}), bf16[512,4,128]{2,0,1:T(8,128)(2,1)S(1)}, u32[]{:S(2)}, u32[]{:S(2)}) %all-to-all-start.1) | async-done | bytes 524320 | tf_op jit(solution)/shard_map/all_to_all | solution.py:470
  111.5 0.8 copy.36
  112.3 0.0 copy-done
  112.3 1.3 %copy.37 = bf16[2048,512]{1,0:T(8,128)(2,1)} copy(bf16[2048,512]{1,0:T(8,128)(2,1)S(1)} %copy-done) | data formatting | bytes 4194304
  (2 shorter events, 0.0 us)
Async XLA Ops:
  64.0 3.8 %copy-start.1 = (bf16[512,512]{1,0:T(8,128)(2,1)S(1)}, bf16[512,512]{1,0:T(8,128)(2,1)}, u32[]{:S(2)}) copy-start(bf16[512,512]{1,0:T(8,128)(2,1)} %get-tuple-element.5) | copy-start | bytes 1572868
  64.0 29.5 %all-to-all-start = ((bf16[4,512,512]{2,1,0:T(8,128)(2,1)}), bf16[4,512,512]{2,1,0:T(8,128)(2,1)S(1)}, u32[]{:S(2)}, u32[]{:S(2)}) async-start(bf16[4,512,512]{2,1,0:T(8,128)(2,1)} %bitcast.18), calls=%async_computation | async-start | bytes 4194304 | tf_op jit(solution)/shard_map/all_to_all | solution.py:32
  67.8 27.0 %copy-start.4 = (f32[512]{0:T(512)S(1)}, f32[512]{0:T(512)}, u32[]{:S(2)}) copy-start(f32[512]{0:T(512)} %param.35) | copy-start | bytes 6148
  67.8 27.0 %copy-start.5 = (f32[512]{0:T(512)S(1)}, f32[512]{0:T(512)}, u32[]{:S(2)}) copy-start(f32[512]{0:T(512)} %param.33) | copy-start | bytes 6148
  94.7 2.9 %copy-start.2 = (f32[512]{0:T(512)S(1)}, f32[512]{0:T(512)}, u32[]{:S(2)}) copy-start(f32[512]{0:T(512)} %param.37) | copy-start | bytes 6148
  94.7 2.9 %copy-start.3 = (f32[512]{0:T(512)S(1)}, f32[512]{0:T(512)}, u32[]{:S(2)}) copy-start(f32[512]{0:T(512)} %param.36) | copy-start | bytes 6148
  97.7 14.6 %copy-start = (bf16[2048,512]{1,0:T(8,128)(2,1)S(1)}, bf16[2048,512]{1,0:T(8,128)(2,1)}, u32[]{:S(2)}) copy-start(bf16[2048,512]{1,0:T(8,128)(2,1)} %get-tuple-element.13) | copy-start | bytes 6291460
  100.0 11.5 %all-to-all-start.1 = ((bf16[512,4,128]{2,0,1:T(8,128)(2,1)}), bf16[512,4,128]{2,0,1:T(8,128)(2,1)S(1)}, u32[]{:S(2)}, u32[]{:S(2)}) async-start(bf16[512,4,128]{2,0,1:T(8,128)(2,1)} %copy_bitcast_fusion), calls=%async_computation.1 | async-start | bytes 1048576 | tf_op jit(solution)/shard_map/all_to_all | solution.py:470

commit v3 on v2

--- a/solution.py
+++ b/solution.py
@@ -16,21 +16,14 @@
 
 TO_RIGHT, TO_LEFT, RELAY_RIGHT, RELAY_LEFT = 0, 4, 8, 10
 FORWARD, BACKWARD, COARSE, PICKED = 12, 16, 20, 21
-SLOTS = 24
-L_NODES, L_EDGES, L_IN, L_OUT, L_RESULT = 0, 1, 2, 3, 4
-LOCALS = 12
-
-
-def in_blocks(array, dim, count):
-    lengths = array.shape
-    blocks = array.reshape(*lengths[:dim], count, lengths[dim] // count, *lengths[dim + 1 :])
-    return jnp.moveaxis(blocks, dim, 0)
-
-
-def sent_and_summed(array, axis, dim):
-    blocks = in_blocks(array, dim, lax.axis_size(axis))
-    arrived = lax.all_to_all(blocks, axis, split_axis=0, concat_axis=0, tiled=True)
-    return arrived.astype(jnp.float32).sum(axis=0)
+PIECES = 2
+PASS_RIGHT, PASS_LEFT = 24, 26
+PLAIN_RIGHT, PLAIN_LEFT = 28, 30
+SUM_RIGHT, SUM_LEFT = 32, 34
+NEW = 36
+SLOTS = NEW + 6 * PIECES
+L_NODES, L_EDGES, L_IN, L_OUT, L_NODE_IN, L_NODE_OUT, L_RESULT, L_OWN = 0, 1, 2, 3, 4, 5, 6, 7
+LOCALS = 8
 
 
 def normalize(output, norm_gain, norm_shift):
@@ -45,15 +38,12 @@
     return half + half * jnp.tanh(half)
 
 
-def one_hot_rows(ids_ref, out_ref, offset=None):
+def one_hot_rows(line_of, out_ref):
     rows, width = out_ref.shape
     lane = lax.broadcasted_iota(jnp.int32, (LANES, LANES), 1)
 
     def block(r, carry):
-        line = ids_ref[pl.ds(r, 1), :]
-        if offset is not None:
-            line = line + offset(r)
-        ids = jnp.broadcast_to(line, (LANES, LANES)).T
+        ids = jnp.broadcast_to(line_of(r), (LANES, LANES)).T
         here = pl.ds(pl.multiple_of(r * LANES, LANES), LANES)
         for k in range(width // LANES):
             out_ref[here, k * LANES : (k + 1) * LANES] = jnp.where(
@@ -79,9 +69,14 @@
     b_out_ref,
     gain_ref,
     shift_ref,
+    w_node_in_ref,
+    b_node_in_ref,
+    w_node_out_ref,
+    b_node_out_ref,
+    node_gain_ref,
+    node_shift_ref,
+    nodes_out_ref,
     edges_out_ref,
-    sums_ref,
-    own_rows_ref,
     table,
     outgoing,
     everyone,
@@ -96,6 +91,14 @@
     sent,
     w_in,
     w_out,
+    w_node_in,
+    w_node_out,
+    sums,
+    passed,
+    plain,
+    summed,
+    pre_node,
+    new,
     send_sem,
     recv_sem,
     local_sem,
@@ -144,10 +147,19 @@
     edges_in = pltpu.make_async_copy(edges_ref, edges, local_sem.at[L_EDGES])
     w_in_in = pltpu.make_async_copy(w_in_ref, w_in, local_sem.at[L_IN])
     w_out_in = pltpu.make_async_copy(w_out_ref, w_out, local_sem.at[L_OUT])
-    for c in (nodes_in, edges_in, w_in_in, w_out_in):
+    w_node_in_in = pltpu.make_async_copy(w_node_in_ref, w_node_in, local_sem.at[L_NODE_IN])
+    w_node_out_in = pltpu.make_async_copy(w_node_out_ref, w_node_out, local_sem.at[L_NODE_OUT])
+    for c in (nodes_in, edges_in, w_in_in, w_out_in, w_node_in_in, w_node_out_in):
         c.start()
 
-    one_hot_rows(halo_ref, hot_halo)
+    lines = border // LANES
+
+    def halo_line(r):
+        side, place = lax.div(r, lines), lax.rem(r, lines)
+        both = halo_ref[0, :, pl.ds(pl.multiple_of(place * LANES, LANES), LANES)]
+        return jnp.where(side == 0, both[:1], both[1:])
+
+    one_hot_rows(halo_line, hot_halo)
     pl.semaphore_wait(barrier, patches + 2)
     nodes_in.wait()
 
@@ -223,12 +235,17 @@
 
     lax.fori_loop(0, edge_rows // block, self_block, 0)
 
-    one_hot_rows(receivers_ref, hot_recv)
+    one_hot_rows(lambda r: receivers_ref[pl.ds(r, 1), :], hot_recv)
     per_slot = hot_pick.shape[0] // patches
-    spot = lax.broadcasted_iota(jnp.int32, (1, LANES), 1)
-    one_hot_rows(
-        coarse_ref, hot_pick, lambda r: lax.div(r * LANES + spot, per_slot) * coarse_dev
-    )
+    first_picked = node_rows + 2 * border
+    owner = lax.broadcasted_iota(jnp.int32, (patches, LANES), 0) * coarse_dev
+    spot = lax.broadcasted_iota(jnp.int32, (patches, LANES), 1)
+    for k in range(per_slot):
+        wanted = jnp.broadcast_to(coarse_ref[0, :, k : k + 1], (patches, LANES)) + owner
+        for b in range(hot_pick.shape[1] // LANES):
+            hot_pick[k * patches : (k + 1) * patches, b * LANES : (b + 1) * LANES] = jnp.where(
+                wanted == spot + b * LANES, 1.0, 0.0
+            ).astype(jnp.bfloat16)
 
     def from_left(k):
         return copy_to(rows_of(left, k), rows_of(left, k), TO_RIGHT + k, p, right)
@@ -249,7 +266,6 @@
         everyone.at[pl.ds(0, peers), :], everyone.at[pl.ds(0, peers), :], COARSE, after, h
     )
     all_coarse.wait_recv()
-    first_picked = node_rows + 2 * border
     picked_rows = hot_pick.shape[0]
     picked = table.at[h, pl.ds(first_picked, picked_rows), :]
     table[h, first_picked : first_picked + picked_rows, :] = jnp.dot(
@@ -259,7 +275,13 @@
     for c in pick_copies:
         c.start()
 
-    one_hot_rows(senders_ref, hot_send)
+    def sender_line(r):
+        code = senders_ref[pl.ds(r, 1), :]
+        slot = code - first_picked
+        moved = lax.rem(slot, per_slot) * patches + lax.div(slot, per_slot)
+        return jnp.where(slot >= 0, first_picked + moved, code)
+
+    one_hot_rows(sender_line, hot_send)
 
     for k in (2, 3):
         from_left(k).wait_recv()
@@ -329,95 +351,155 @@
     edges_done.start()
 
     share_rows = node_rows // shards
-
-    def sum_block(j, carry):
-        start = pl.multiple_of(j * share_rows, share_rows)
-        node = start + lax.broadcasted_iota(jnp.int32, (share_rows, LANES), 0)
-        for k in range(edge_rows // LANES):
-            ids = jnp.broadcast_to(receivers_ref[k : k + 1, :], (share_rows, LANES))
-            hot_recv[:share_rows, k * LANES : (k + 1) * LANES] = jnp.where(
+    half = share_rows // 2
+    size = half // PIECES
+
+    def sum_at(j):
+        node = j * share_rows + lax.broadcasted_iota(jnp.int32, (share_rows, LANES), 0)
+
+        def line(k, carry):
+            ids = jnp.broadcast_to(receivers_ref[pl.ds(k, 1), :], (share_rows, LANES))
+            hot_recv[:share_rows, pl.ds(pl.multiple_of(k * LANES, LANES), LANES)] = jnp.where(
                 node == ids, 1.0, 0.0
             ).astype(jnp.bfloat16)
-        sums_ref[pl.ds(start, share_rows), :] = jnp.dot(
+            return carry
+
+        lax.fori_loop(0, edge_rows // LANES, line, 0)
+        sums[j] = jnp.dot(
             hot_recv[:share_rows, :edge_rows], sent[...], preferred_element_type=jnp.float32
         ).astype(jnp.bfloat16)
-        return carry
-
-    lax.fori_loop(0, shards, sum_block, 0)
-    mine = pl.ds(pl.multiple_of(h * share_rows, share_rows), share_rows)
-    for c in range(columns // LANES):
-        own_rows_ref[:, c * LANES : (c + 1) * LANES] = table[c, mine, :]
+
+    def piece_rows(k):
+        return pl.ds(k * size, size)
+
+    def piece_copy(source, target, slot, g):
+        return copy_to(source, target, slot, p, g)
+
+    sum_at(far)
+    ring = []
+    for k in range(PIECES):
+        ring.append(piece_copy(sums.at[far, piece_rows(k), :], passed.at[0, piece_rows(k), :], PASS_RIGHT + k, right))
+        ring.append(piece_copy(sums.at[far, piece_rows(PIECES + k), :], passed.at[1, piece_rows(k), :], PASS_LEFT + k, left))
+    for c in ring:
+        c.start()
+    sum_at(right)
+    plain_right = [
+        piece_copy(sums.at[right, piece_rows(PIECES + k), :], plain.at[0, piece_rows(k), :], PLAIN_RIGHT + k, right)
+        for k in range(PIECES)
+    ]
+    for c in plain_right:
+        c.start()
+    sum_at(left)
+    plain_left = [
+        piece_copy(sums.at[left, piece_rows(k), :], plain.at[1, piece_rows(k), :], PLAIN_LEFT + k, left)
+        for k in range(PIECES)
+    ]
+    for c in plain_left:
+        c.start()
+
+    sum_copies = []
+    for k in range(PIECES):
+        here = piece_rows(k)
+        other = piece_rows(PIECES + k)
+        piece_copy(passed.at[0, here, :], passed.at[0, here, :], PASS_RIGHT + k, right).wait_recv()
+        sums[right, k * size : (k + 1) * size, :] = (
+            sums[right, k * size : (k + 1) * size, :].astype(jnp.float32)
+            + passed[0, k * size : (k + 1) * size, :].astype(jnp.float32)
+        ).astype(jnp.bfloat16)
+        c = piece_copy(sums.at[right, here, :], summed.at[0, here, :], SUM_RIGHT + k, right)
+        c.start()
+        sum_copies.append(c)
+        piece_copy(passed.at[1, here, :], passed.at[1, here, :], PASS_LEFT + k, left).wait_recv()
+        sums[left, half + k * size : half + (k + 1) * size, :] = (
+            sums[left, half + k * size : half + (k + 1) * size, :].astype(jnp.float32)
+            + passed[1, k * size : (k + 1) * size, :].astype(jnp.float32)
+        ).astype(jnp.bfloat16)
+        c = piece_copy(sums.at[left, other, :], summed.at[1, here, :], SUM_LEFT + k, left)
+        c.start()
+        sum_copies.append(c)
+
+    sum_at(h)
+    w_node_in_in.wait()
+    w_node_out_in.wait()
+
+    def own_rows(first, count):
+        there = pl.ds(pl.multiple_of(h * share_rows + first, count), count)
+        return jnp.concatenate([table[c, there, :] for c in range(columns // LANES)], axis=1)
+
+    pre_node[...] = (
+        jnp.dot(
+            own_rows(0, share_rows), w_node_in[:columns, :], preferred_element_type=jnp.float32
+        )
+        + b_node_in_ref[...]
+    )
+
+    new_copies = []
+    home = []
+    for k in range(PIECES):
+        here = piece_rows(k)
+        spans = ((k * size, 0), (half + k * size, 1))
+        piece_copy(summed.at[0, here, :], summed.at[0, here, :], SUM_RIGHT + k, right).wait_recv()
+        piece_copy(summed.at[1, here, :], summed.at[1, here, :], SUM_LEFT + k, left).wait_recv()
+        piece_copy(plain.at[0, here, :], plain.at[0, here, :], PLAIN_RIGHT + k, right).wait_recv()
+        piece_copy(plain.at[1, here, :], plain.at[1, here, :], PLAIN_LEFT + k, left).wait_recv()
+        gathered = jnp.concatenate(
+            [
+                (
+                    sums[h, first : first + size, :].astype(jnp.float32)
+                    + summed[side, k * size : (k + 1) * size, :].astype(jnp.float32)
+                    + plain[1 - side, k * size : (k + 1) * size, :].astype(jnp.float32)
+                ).astype(jnp.bfloat16)
+                for first, side in spans
+            ],
+            axis=0,
+        )
+        value = jnp.concatenate([pre_node[first : first + size, :] for first, side in spans], axis=0)
+        value = value + jnp.dot(
+            gathered, w_node_in[columns:, :], preferred_element_type=jnp.float32
+        )
+        active = silu(value).astype(jnp.bfloat16)
+        output = jnp.dot(active, w_node_out[...], preferred_element_type=jnp.float32) + b_node_out_ref[...]
+        update = normalize(output, node_gain_ref[...], node_shift_ref[...])
+        old = jnp.concatenate([own_rows(first, size) for first, side in spans], axis=0)
+        result = (old.astype(jnp.float32) + update).astype(jnp.bfloat16)
+        for c in range(columns // LANES):
+            for n, (first, side) in enumerate(spans):
+                new[c, first : first + size, :] = result[
+                    n * size : (n + 1) * size, c * LANES : (c + 1) * LANES
+                ]
+        for n, (first, side) in enumerate(spans):
+            there = pl.ds(pl.multiple_of(h * share_rows + first, size), size)
+            for m, g in enumerate((far, right, left)):
+                c = piece_copy(
+                    new.at[g, pl.ds(first, size), :],
+                    nodes_out_ref.at[there, :],
+                    NEW + (k * 2 + n) * 3 + m,
+                    g,
+                )
+                c.start()
+                new_copies.append(c)
+    share_there = pl.ds(pl.multiple_of(h * share_rows, share_rows), share_rows)
+    home = pltpu.make_async_copy(new.at[h], nodes_out_ref.at[share_there, :], local_sem.at[L_OWN])
+    home.start()
 
     for c in to_right + to_left + relay_right + relay_left + pick_copies:
         c.wait_send()
     for c in halos[0] + halos[1] + halos[2]:
         c.wait_send()
     all_coarse.wait_send()
+    for c in ring + plain_right + plain_left + sum_copies + new_copies:
+        c.wait_send()
     edges_done.wait()
-
-
-def layer_stage(nodes, edges, senders, receivers, halo_rows, coarse_rows, edge_count, w_in, b_in, w_out, b_out, gain, shift):
-    edge_rows, columns = edges.shape
-    node_rows = nodes.shape[0]
-    border = halo_rows.shape[2]
-    picked = coarse_rows.shape[1] * coarse_rows.shape[2]
-    total = node_rows + 2 * border + picked
-    shards = lax.axis_size("hidden")
-    patches = lax.axis_size("patch")
-    vmem = pl.BlockSpec(memory_space=pltpu.VMEM)
-    smem = pl.BlockSpec(memory_space=pltpu.SMEM)
-    far_away = pl.BlockSpec(memory_space=pl.ANY)
-    bf16 = jnp.bfloat16
-    parts = columns // LANES
-    return pl.pallas_call(
-        lambda *refs: layer_kernel(COARSE_DEV, *refs),
-        out_shape=(
-            jax.ShapeDtypeStruct((edge_rows, columns), bf16),
-            jax.ShapeDtypeStruct((node_rows, columns), bf16),
-            jax.ShapeDtypeStruct((node_rows // shards, columns), bf16),
-        ),
-        in_specs=[smem, far_away, far_away, vmem, vmem, vmem, vmem, far_away, vmem, far_away, vmem, vmem, vmem],
-        out_specs=(far_away, vmem, vmem),
-        scratch_shapes=[
-            pltpu.VMEM((parts, total, LANES), bf16),
-            pltpu.VMEM((parts, 2 * border, LANES), bf16),
-            pltpu.VMEM((patches * COARSE_DEV, LANES), bf16),
-            pltpu.VMEM((2 * border, node_rows), bf16),
-            pltpu.VMEM((edge_rows, total), bf16),
-            pltpu.VMEM((edge_rows, node_rows), bf16),
-            pltpu.VMEM((picked, patches * COARSE_DEV), bf16),
-            pltpu.VMEM((parts, edge_rows, LANES), bf16),
-            pltpu.VMEM((parts, edge_rows, LANES), bf16),
-            pltpu.VMEM((edge_rows, columns), jnp.float32),
-            pltpu.VMEM((edge_rows, columns), bf16),
-            pltpu.VMEM((edge_rows, columns), bf16),
-            pltpu.VMEM(w_in.shape, bf16),
-            pltpu.VMEM(w_out.shape, bf16),
-            pltpu.SemaphoreType.DMA((SLOTS,)),
-            pltpu.SemaphoreType.DMA((SLOTS,)),
-            pltpu.SemaphoreType.DMA((LOCALS,)),
-        ],
-        compiler_params=pltpu.CompilerParams(
-            vmem_limit_bytes=67043328, collective_id=0, has_side_effects=True
-        ),
-    )(
-        edge_count,
-        nodes,
-        edges,
-        senders.reshape(-1, LANES),
-        receivers.reshape(-1, LANES),
-        halo_rows.reshape(-1, LANES),
-        coarse_rows.reshape(-1, LANES),
-        w_in,
-        b_in.reshape(1, -1),
-        w_out,
-        b_out.reshape(1, -1),
-        gain.reshape(1, -1),
-        shift.reshape(1, -1),
-    )
-
-
-def local(
+    home.wait()
+    for k in range(PIECES):
+        for n, first in enumerate((k * size, half + k * size)):
+            for m, g in enumerate((far, left, right)):
+                there = pl.ds(pl.multiple_of(g * share_rows + first, size), size)
+                landed = nodes_out_ref.at[there, :]
+                piece_copy(landed, landed, NEW + (k * 2 + n) * 3 + m, right).wait_recv()
+
+
+def layer_stage(
     nodes,
     edges,
     senders,
@@ -438,42 +520,88 @@
     node_gain,
     node_shift,
 ):
-    columns = edges.shape[1]
-    edges_out, summed, own_rows = layer_stage(
+    edge_rows, columns = edges.shape
+    node_rows = nodes.shape[0]
+    border = halo_rows.shape[2]
+    picked = coarse_rows.shape[1] * coarse_rows.shape[2]
+    total = node_rows + 2 * border + picked
+    shards = lax.axis_size("hidden")
+    patches = lax.axis_size("patch")
+    share_rows = node_rows // shards
+    vmem = pl.BlockSpec(memory_space=pltpu.VMEM)
+    smem = pl.BlockSpec(memory_space=pltpu.SMEM)
+    far_away = pl.BlockSpec(memory_space=pl.ANY)
+    bf16 = jnp.bfloat16
+    parts = columns // LANES
+    network = [far_away, vmem, far_away, vmem, vmem, vmem]
+
+    def row(v):
+        return v.reshape(1, -1)
+
+    return pl.pallas_call(
+        lambda *refs: layer_kernel(COARSE_DEV, *refs),
+        out_shape=(
+            jax.ShapeDtypeStruct(nodes.shape, bf16),
+            jax.ShapeDtypeStruct((edge_rows, columns), bf16),
+        ),
+        in_specs=[smem, far_away, far_away, vmem, vmem, vmem, vmem, *network, *network],
+        out_specs=(far_away, far_away),
+        scratch_shapes=[
+            pltpu.VMEM((parts, total, LANES), bf16),
+            pltpu.VMEM((parts, 2 * border, LANES), bf16),
+            pltpu.VMEM((patches * COARSE_DEV, LANES), bf16),
+            pltpu.VMEM((2 * border, node_rows), bf16),
+            pltpu.VMEM((edge_rows, total), bf16),
+            pltpu.VMEM((edge_rows, node_rows), bf16),
+            pltpu.VMEM((picked, patches * COARSE_DEV), bf16),
+            pltpu.VMEM((parts, edge_rows, LANES), bf16),
+            pltpu.VMEM((parts, edge_rows, LANES), bf16),
+            pltpu.VMEM((edge_rows, columns), jnp.float32),
+            pltpu.VMEM((edge_rows, columns), bf16),
+            pltpu.VMEM((edge_rows, columns), bf16),
+            pltpu.VMEM(w_edge_in.shape, bf16),
+            pltpu.VMEM(w_edge_out.shape, bf16),
+            pltpu.VMEM(w_node_in.shape, bf16),
+            pltpu.VMEM(w_node_out.shape, bf16),
+            pltpu.VMEM((shards, share_rows, columns), bf16),
+            pltpu.VMEM((2, share_rows // 2, columns), bf16),
+            pltpu.VMEM((2, share_rows // 2, columns), bf16),
+            pltpu.VMEM((2, share_rows // 2, columns), bf16),
+            pltpu.VMEM((share_rows, columns), jnp.float32),
+            pltpu.VMEM((parts, share_rows, LANES), bf16),
+            pltpu.SemaphoreType.DMA((SLOTS,)),
+            pltpu.SemaphoreType.DMA((SLOTS,)),
+            pltpu.SemaphoreType.DMA((LOCALS,)),
+        ],
+        compiler_params=pltpu.CompilerParams(
+            vmem_limit_bytes=67043328, collective_id=0, has_side_effects=True
+        ),
+    )(
+        edge_count,
         nodes,
         edges,
-        senders,
-        receivers,
+        senders.reshape(-1, LANES),
+        receivers.reshape(-1, LANES),
         halo_rows,
         coarse_rows,
-        edge_count,
         w_edge_in,
-        b_edge_in,
+        row(b_edge_in),
         w_edge_out,
-        b_edge_out,
-        edge_gain,
-        edge_shift,
+        row(b_edge_out),
+        row(edge_gain),
+        row(edge_shift),
+        w_node_in,
+        row(b_node_in),
+        w_node_out,
+        row(b_node_out),
+        row(node_gain),
+        row(node_shift),
     )
-    aggregated = sent_and_summed(summed, "hidden", 0)
-    pre_active = jnp.dot(own_rows, w_node_in[:columns], preferred_element_type=jnp.float32)
-    pre_active = (
-        pre_active
-        + jnp.dot(
-            aggregated.astype(jnp.bfloat16), w_node_in[columns:], preferred_element_type=jnp.float32
-        )
-        + b_node_in
-    )
-    active = jax.nn.silu(pre_active).astype(jnp.bfloat16)
-    output = jnp.dot(active, w_node_out, preferred_element_type=jnp.float32) + b_node_out
-    update = normalize(output, node_gain, node_shift)
-    new_rows = (own_rows.astype(jnp.float32) + update).astype(jnp.bfloat16)
-    nodes_out = lax.all_to_all(new_rows, "hidden", split_axis=1, concat_axis=0, tiled=True)
-    return (nodes_out, edges_out)
 
 
 def solution(mesh):
     return jax.shard_map(
-        local,
+        layer_stage,
         mesh=mesh,
         in_specs=(
             P("patch", "hidden"),

time: 115 us -> 88.4 us (0.77)
  waiting for transfers between devices: 31.3 us -> 0 us
  Pallas kernels: 60 us -> 80.6 us
  starting transfers between devices: 7.22 us -> 0 us
  matrix products: 5.1 us -> 0 us
  other arithmetic: 3.82 us -> 0 us
  local copies, waits for them, and re-layouts: 4.86 us -> 6.28 us
    all_to_all x2 -> x0, waiting for transfers between devices: 31.3 us -> none  [the longest x1 23.2 us: sent_and_summed(): lax.all_to_all(blocks, axis, split_axis=0, concat_axis=0, tiled=True)]
    pallas_call x1, Pallas kernels: 60 us -> 80.6 us  [layer_stage(): pl.pallas_call(lambda *refs: layer_kernel(COARSE_DEV, *refs), out_shape=(...]
    all_to_all x2 -> x0, starting transfers between devices: 7.22 us -> none  [the longest x1 3.75 us: sent_and_summed(): lax.all_to_all(blocks, axis, split_axis=0, concat_axis=0, tiled=True)]
    dot_general x2 -> x0, matrix products: 5.1 us -> none  [the longest x1 2.65 us: local(): jnp.dot(active, w_node_out, preferred_element_type=jnp.float32) + b_node_out]
    unnamed x15 -> x3, local copies, waits for them, and re-layouts: 2.9 us -> 6.28 us
    all_to_all x1 -> x0, other arithmetic: 2.3 us -> none  [local(): lax.all_to_all(new_rows, 'hidden', split_axis=1, concat_axis=0, tiled=True)]
    reshape x2 -> x0, local copies, waits for them, and re-layouts: 1.96 us -> none  [the longest x1 1.31 us: layer_stage(): halo_rows.reshape(-1, LANES)]
    reduce_sum x2 -> x0, other arithmetic: 1.5 us -> none  [the longest x1 1.24 us: sent_and_summed(): return arrived.astype(jnp.float32).sum(axis=0)]
  transfers between devices with their start and end apart: 2 -> 0, of which waited for: 2 -> 0; matrix products, arithmetic and copies ran while one was open for 2% -> 0% of each run, Pallas kernels for 0% -> 0%
where the time goes in v3:
time: 88.4 us; the launch traced here: 88.1 us
  Pallas kernels  80.6 us (91%)
  local copies, waits for them, and re-layouts  6.28 us (7%)
  between operations  1.29 us (1%)
    pallas_call x1, Pallas kernels, layer_stage(): pl.pallas_call(lambda *refs: layer_kernel(COARSE_DEV, *refs), out_shape=(...  80.6 us
    unnamed x3, local copies, waits for them, and re-layouts  6.28 us

profile of v3, /device:TPU:0, one launch (start us, length us, event | category | flops | bytes accessed | tf_op | source)
XLA Modules:
  0.0 88.1 jit_solution(15354481235344027351)
XLA Ops:
  1.3 1.4 %copy.21.refs_6_ = s32[1,32,8]{2,1,0:T(8,128)} copy(s32[1,32,8]{1,2,0:T(8,128)} %param.24) | data formatting | bytes 2048 | tf_op args[5]
  2.6 80.6 %shard_map.194 = (bf16[2048,128]{1,0:T(8,128)(2,1)}, bf16[2048,512]{1,0:T(8,128)(2,1)}) custom-call(s32[1]{0:T(128)S(6)} %copy.24.refs_0_, bf16[2048,128]{1,0:T(8,128)(2,1)} %refs_1_.1, bf16[2048,512]{1,0:T(8,128)(2,1)} %refs_2_.1, s32[16,128]{1,0:T(8,128)} %bitcast.10, s32[16,128]{1,0:T(8,128)} %bitcast.11, s32[1,2,1024]{2,1,0:T(2,128)} %refs_5_.1, ...), custom_call_target="tpu_custom_call" | custom-call | tf_op jit(solution)/shard_map/pallas_call | solution.py:541
  83.2 1.9 %copy.25 = bf16[2048,128]{1,0:T(8,128)(2,1)} copy(bf16[2048,128]{1,0:T(8,128)(2,1)} %get-tuple-element.4) | data formatting | bytes 1048576
  85.1 3.0 %copy.26 = bf16[2048,512]{1,0:T(8,128)(2,1)} copy(bf16[2048,512]{1,0:T(8,128)(2,1)} %get-tuple-element.5) | data formatting | bytes 4194304

commit v4 on v3

--- a/solution.py
+++ b/solution.py
@@ -8,6 +8,7 @@
 COARSE_DEV = 64
 LANES = 128
 ROW_BLOCK = 512
+LONG_BLOCK = 1024
 CHUNKS = 4
 MESH = pl.DeviceIdType.MESH
 
@@ -16,11 +17,11 @@
 
 TO_RIGHT, TO_LEFT, RELAY_RIGHT, RELAY_LEFT = 0, 4, 8, 10
 FORWARD, BACKWARD, COARSE, PICKED = 12, 16, 20, 21
-PIECES = 2
-PASS_RIGHT, PASS_LEFT = 24, 26
-PLAIN_RIGHT, PLAIN_LEFT = 28, 30
-SUM_RIGHT, SUM_LEFT = 32, 34
-NEW = 36
+PIECES = 4
+PASS_RIGHT, PASS_LEFT = 24, 24 + PIECES
+PLAIN_RIGHT, PLAIN_LEFT = 24 + 2 * PIECES, 24 + 3 * PIECES
+SUM_RIGHT, SUM_LEFT = 24 + 4 * PIECES, 24 + 5 * PIECES
+NEW = 24 + 6 * PIECES
 SLOTS = NEW + 6 * PIECES
 L_NODES, L_EDGES, L_IN, L_OUT, L_NODE_IN, L_NODE_OUT, L_RESULT, L_OWN = 0, 1, 2, 3, 4, 5, 6, 7
 LOCALS = 8
@@ -38,20 +39,21 @@
     return half + half * jnp.tanh(half)
 
 
-def one_hot_rows(line_of, out_ref):
-    rows, width = out_ref.shape
-    lane = lax.broadcasted_iota(jnp.int32, (LANES, LANES), 1)
-
-    def block(r, carry):
-        ids = jnp.broadcast_to(line_of(r), (LANES, LANES)).T
-        here = pl.ds(pl.multiple_of(r * LANES, LANES), LANES)
-        for k in range(width // LANES):
-            out_ref[here, k * LANES : (k + 1) * LANES] = jnp.where(
-                ids == lane + k * LANES, 1.0, 0.0
-            ).astype(jnp.bfloat16)
-        return carry
-
-    lax.fori_loop(0, rows // LANES, block, 0)
+def one_hot(line_of, first, lines, low, high):
+    lane = low + lax.broadcasted_iota(jnp.int32, (LANES, LANES), 1)
+    rows = []
+    for r in range(lines):
+        ids = jnp.broadcast_to(line_of(first + r), (LANES, LANES)).T
+        rows.append(
+            jnp.concatenate(
+                [
+                    jnp.where(ids == lane + k, 1.0, 0.0).astype(jnp.bfloat16)
+                    for k in range(0, high - low, LANES)
+                ],
+                axis=1,
+            )
+        )
+    return jnp.concatenate(rows, axis=0)
 
 
 def layer_kernel(
@@ -80,14 +82,10 @@
     table,
     outgoing,
     everyone,
-    hot_halo,
-    hot_send,
-    hot_recv,
     hot_pick,
     send_rows,
     recv_rows,
     pre,
-    edges,
     sent,
     w_in,
     w_out,
@@ -97,12 +95,11 @@
     passed,
     plain,
     summed,
-    pre_node,
-    new,
     send_sem,
     recv_sem,
     local_sem,
 ):
+    edges = edges_out_ref
     p, h = lax.axis_index("patch"), lax.axis_index("hidden")
     patches, shards = lax.axis_size("patch"), lax.axis_size("hidden")
     right, left, far = (lax.rem(h + s, shards) for s in (1, shards - 1, 2))
@@ -159,13 +156,15 @@
         both = halo_ref[0, :, pl.ds(pl.multiple_of(place * LANES, LANES), LANES)]
         return jnp.where(side == 0, both[:1], both[1:])
 
-    one_hot_rows(halo_line, hot_halo)
+    def loop(count, body):
+        lax.fori_loop(0, count, lambda i, carry: (body(i), carry)[1], 0)
+
     pl.semaphore_wait(barrier, patches + 2)
     nodes_in.wait()
 
     to_right = [copy_to(rows_of(h, k), rows_of(h, k), TO_RIGHT + k, p, right) for k in range(CHUNKS)]
     to_left = [copy_to(rows_of(h, k), rows_of(h, k), TO_LEFT + k, p, left) for k in range(CHUNKS)]
-    for a, b in ((0, 2), (1, 3), (2, 0), (3, 1)):
+    for a, b in ((0, 1), (1, 0), (2, 3), (3, 2)):
         to_right[a].start()
         to_left[b].start()
 
@@ -179,25 +178,29 @@
     lax.fori_loop(1, patches, share, 0)
     everyone[slot_rows, :] = own_coarse[...]
 
-    border_blocks = 2 * border // min(ROW_BLOCK, 2 * border)
-
-    def send_halo(parts, names):
-        width = len(parts) * LANES
-        source = jnp.concatenate([table[c, :node_rows, :] for c in parts], axis=1)
-        size = 2 * border // border_blocks
-
-        def piece(i, carry):
-            here = pl.ds(pl.multiple_of(i * size, size), size)
+    long_block = min(LONG_BLOCK, edge_rows, 2 * border)
+    long_lines = long_block // LANES
+    border_blocks = 2 * border // long_block
+    gather_blocks = edge_rows // long_block
+
+    def side(parts, low, high):
+        return jnp.concatenate([table[c, low:high, :] for c in parts], axis=1)
+
+    def halo(parts, names, low, high, add):
+        def piece(i):
+            here = pl.ds(pl.multiple_of(i * long_block, long_block), long_block)
             result = jnp.dot(
-                hot_halo[here, :],
-                jnp.concatenate([table[c, :node_rows, :] for c in parts], axis=1),
+                one_hot(halo_line, i * long_lines, long_lines, low, high),
+                side(parts, low, high),
                 preferred_element_type=jnp.float32,
             ).astype(jnp.bfloat16)
             for n, name in enumerate(names):
-                outgoing[name, here, :] = result[:, n * LANES : (n + 1) * LANES]
-            return carry
-
-        lax.fori_loop(0, border_blocks, piece, 0)
+                value = result[:, n * LANES : (n + 1) * LANES]
+                outgoing[name, here, :] = outgoing[name, here, :] + value if add else value
+
+        loop(border_blocks, piece)
+
+    def send_halo(parts, names):
         copies = []
         for part, name in zip(parts, names):
             back = copy_to(
@@ -220,10 +223,22 @@
         return copies
 
     halos = {}
+    edge_lines = edge_rows // LANES
+    middle = node_rows // 2
+    halo((h,), (0,), 0, node_rows, False)
     halos[0] = send_halo((h,), (0,))
 
     edges_in.wait()
     w_in_in.wait()
+
+    per_slot = hot_pick.shape[0] // patches
+    first_picked = node_rows + 2 * border
+
+    def sender_line(r):
+        code = senders_ref[pl.ds(r, 1), :]
+        slot = code - first_picked
+        moved = lax.rem(slot, per_slot) * patches + lax.div(slot, per_slot)
+        return jnp.where(slot >= 0, first_picked + moved, code)
 
     def self_block(i, carry):
         here = pl.ds(pl.multiple_of(i * block, block), block)
@@ -235,13 +250,11 @@
 
     lax.fori_loop(0, edge_rows // block, self_block, 0)
 
-    one_hot_rows(lambda r: receivers_ref[pl.ds(r, 1), :], hot_recv)
-    per_slot = hot_pick.shape[0] // patches
-    first_picked = node_rows + 2 * border
     owner = lax.broadcasted_iota(jnp.int32, (patches, LANES), 0) * coarse_dev
     spot = lax.broadcasted_iota(jnp.int32, (patches, LANES), 1)
     for k in range(per_slot):
-        wanted = jnp.broadcast_to(coarse_ref[0, :, k : k + 1], (patches, LANES)) + owner
+        line = coarse_ref[0, k : k + 1, :]
+        wanted = jnp.broadcast_to(line, (LANES, patches)).T + owner
         for b in range(hot_pick.shape[1] // LANES):
             hot_pick[k * patches : (k + 1) * patches, b * LANES : (b + 1) * LANES] = jnp.where(
                 wanted == spot + b * LANES, 1.0, 0.0
@@ -253,14 +266,44 @@
     def from_right(k):
         return copy_to(rows_of(right, k), rows_of(right, k), TO_LEFT + k, p, left)
 
-    relay_right = [copy_to(rows_of(left, k), rows_of(left, k), RELAY_RIGHT + k, p, right) for k in (0, 1)]
-    relay_left = [copy_to(rows_of(right, k + 2), rows_of(right, k + 2), RELAY_LEFT + k, p, left) for k in (0, 1)]
-    for k in (0, 1):
-        from_left(k).wait_recv()
+    relay_right = [copy_to(rows_of(left, 2 * k), rows_of(left, 2 * k), RELAY_RIGHT + k, p, right) for k in (0, 1)]
+    relay_left = [copy_to(rows_of(right, 2 * k + 1), rows_of(right, 2 * k + 1), RELAY_LEFT + k, p, left) for k in (0, 1)]
+
+    def near_half(k):
+        for c in (2 * k, 2 * k + 1):
+            from_left(c).wait_recv()
+            from_right(c).wait_recv()
         relay_right[k].start()
-        from_right(k + 2).wait_recv()
         relay_left[k].start()
 
+    def far_half(k):
+        copy_to(rows_of(far, 2 * k), rows_of(far, 2 * k), RELAY_RIGHT + k, p, right).wait_recv()
+        copy_to(rows_of(far, 2 * k + 1), rows_of(far, 2 * k + 1), RELAY_LEFT + k, p, left).wait_recv()
+
+    def gather(line_of, low, high, parts, into, add):
+        def piece(i):
+            here = pl.ds(pl.multiple_of(i * long_block, long_block), long_block)
+            result = jnp.dot(
+                one_hot(line_of, i * long_lines, long_lines, low, high),
+                side(parts, low, high),
+                preferred_element_type=jnp.float32,
+            ).astype(jnp.bfloat16)
+            for n, c in enumerate(parts):
+                value = result[:, n * LANES : (n + 1) * LANES]
+                into[c, here, :] = into[c, here, :] + value if add else value
+
+        loop(gather_blocks, piece)
+
+    def receiver_line(r):
+        return receivers_ref[pl.ds(r, 1), :]
+
+    near, pair = (left, right), (h, far)
+    total_rows = table.shape[1]
+    near_half(0)
+    halo(near, (1, 2), 0, middle, False)
+    gather(receiver_line, 0, middle, near, recv_rows, False)
+    gather(sender_line, 0, middle, near, send_rows, False)
+    near_half(1)
     peers = (patches - 1) * coarse_dev
     all_coarse = copy_to(
         everyone.at[pl.ds(0, peers), :], everyone.at[pl.ds(0, peers), :], COARSE, after, h
@@ -275,54 +318,26 @@
     for c in pick_copies:
         c.start()
 
-    def sender_line(r):
-        code = senders_ref[pl.ds(r, 1), :]
-        slot = code - first_picked
-        moved = lax.rem(slot, per_slot) * patches + lax.div(slot, per_slot)
-        return jnp.where(slot >= 0, first_picked + moved, code)
-
-    one_hot_rows(sender_line, hot_send)
-
-    for k in (2, 3):
-        from_left(k).wait_recv()
-        from_right(k - 2).wait_recv()
-    halos[1] = send_halo((left, right), (1, 2))
-
-    def gather(hot, low, high, parts, into, add):
-        def piece(i, carry):
-            here = pl.ds(pl.multiple_of(i * block, block), block)
-            result = jnp.dot(
-                hot[here, low:high],
-                jnp.concatenate([table[c, low:high, :] for c in parts], axis=1),
-                preferred_element_type=jnp.float32,
-            ).astype(jnp.bfloat16)
-            for n, c in enumerate(parts):
-                value = result[:, n * LANES : (n + 1) * LANES]
-                into[c, here, :] = into[c, here, :] + value if add else value
-            return carry
-
-        lax.fori_loop(0, edge_rows // block, piece, 0)
-
-    gather(hot_recv, 0, node_rows, (left, right), recv_rows, False)
-    gather(hot_send, 0, node_rows, (left, right), send_rows, False)
-
-    for k in (0, 1):
-        copy_to(rows_of(far, k), rows_of(far, k), RELAY_RIGHT + k, p, right).wait_recv()
-        copy_to(rows_of(far, k + 2), rows_of(far, k + 2), RELAY_LEFT + k, p, left).wait_recv()
+    halo(near, (1, 2), middle, node_rows, True)
+    halos[1] = send_halo(near, (1, 2))
+    gather(receiver_line, middle, node_rows, near, recv_rows, True)
+    gather(sender_line, middle, node_rows, near, send_rows, True)
+    far_half(0)
+    halo((far,), (3,), 0, middle, False)
+    far_half(1)
+    halo((far,), (3,), middle, node_rows, True)
     halos[2] = send_halo((far,), (3,))
-
-    gather(hot_recv, 0, node_rows, (h, far), recv_rows, False)
-    gather(hot_send, 0, node_rows, (h, far), send_rows, False)
-    total_rows = table.shape[1]
+    gather(receiver_line, 0, node_rows, pair, recv_rows, False)
+    gather(sender_line, 0, node_rows, pair, send_rows, False)
     for c in halos[1]:
         c.wait_recv()
     for n, g in enumerate((left, right, far)):
         landed = table.at[g, pl.ds(first_picked, picked_rows), :]
         copy_to(landed, landed, PICKED + n, p, right).wait_recv()
-    gather(hot_send, node_rows, total_rows, (left, right), send_rows, True)
+    gather(sender_line, node_rows, total_rows, near, send_rows, True)
     for c in halos[0] + halos[2]:
         c.wait_recv()
-    gather(hot_send, node_rows, total_rows, (h, far), send_rows, True)
+    gather(sender_line, node_rows, total_rows, pair, send_rows, True)
 
     w_out_in.wait()
 
@@ -346,27 +361,24 @@
         edges[here, :] = (edges[here, :].astype(jnp.float32) + message).astype(jnp.bfloat16)
         return carry
 
-    lax.fori_loop(0, edge_rows // block, edge_block, 0)
-    edges_done = pltpu.make_async_copy(edges, edges_out_ref, local_sem.at[L_RESULT])
-    edges_done.start()
+    lax.fori_loop(0, edge_rows // block, edge_block, 0, unroll=True)
 
     share_rows = node_rows // shards
+    pre_node = pre.at[pl.ds(0, share_rows), :]
+    new = send_rows.at[:, pl.ds(0, share_rows), :]
     half = share_rows // 2
     size = half // PIECES
 
     def sum_at(j):
         node = j * share_rows + lax.broadcasted_iota(jnp.int32, (share_rows, LANES), 0)
-
-        def line(k, carry):
-            ids = jnp.broadcast_to(receivers_ref[pl.ds(k, 1), :], (share_rows, LANES))
-            hot_recv[:share_rows, pl.ds(pl.multiple_of(k * LANES, LANES), LANES)] = jnp.where(
-                node == ids, 1.0, 0.0
-            ).astype(jnp.bfloat16)
-            return carry
-
-        lax.fori_loop(0, edge_rows // LANES, line, 0)
+        hot = [
+            jnp.where(node == jnp.broadcast_to(receivers_ref[k : k + 1, :], node.shape), 1.0, 0.0)
+            for k in range(edge_lines)
+        ]
         sums[j] = jnp.dot(
-            hot_recv[:share_rows, :edge_rows], sent[...], preferred_element_type=jnp.float32
+            jnp.concatenate([v.astype(jnp.bfloat16) for v in hot], axis=1),
+            sent[...],
+            preferred_element_type=jnp.float32,
         ).astype(jnp.bfloat16)
 
     def piece_rows(k):
@@ -479,8 +491,7 @@
                 c.start()
                 new_copies.append(c)
     share_there = pl.ds(pl.multiple_of(h * share_rows, share_rows), share_rows)
-    home = pltpu.make_async_copy(new.at[h], nodes_out_ref.at[share_there, :], local_sem.at[L_OWN])
-    home.start()
+    nodes_out_ref[share_there, :] = new[h]
 
     for c in to_right + to_left + relay_right + relay_left + pick_copies:
         c.wait_send()
@@ -489,8 +500,6 @@
     all_coarse.wait_send()
     for c in ring + plain_right + plain_left + sum_copies + new_copies:
         c.wait_send()
-    edges_done.wait()
-    home.wait()
     for k in range(PIECES):
         for n, first in enumerate((k * size, half + k * size)):
             for m, g in enumerate((far, left, right)):
@@ -541,23 +550,19 @@
     return pl.pallas_call(
         lambda *refs: layer_kernel(COARSE_DEV, *refs),
         out_shape=(
-            jax.ShapeDtypeStruct(nodes.shape, bf16),
-            jax.ShapeDtypeStruct((edge_rows, columns), bf16),
+            pltpu.VMEM(nodes.shape, bf16),
+            pltpu.VMEM((edge_rows, columns), bf16),
         ),
         in_specs=[smem, far_away, far_away, vmem, vmem, vmem, vmem, *network, *network],
-        out_specs=(far_away, far_away),
+        out_specs=(vmem, vmem),
         scratch_shapes=[
             pltpu.VMEM((parts, total, LANES), bf16),
             pltpu.VMEM((parts, 2 * border, LANES), bf16),
             pltpu.VMEM((patches * COARSE_DEV, LANES), bf16),
-            pltpu.VMEM((2 * border, node_rows), bf16),
-            pltpu.VMEM((edge_rows, total), bf16),
-            pltpu.VMEM((edge_rows, node_rows), bf16),
             pltpu.VMEM((picked, patches * COARSE_DEV), bf16),
             pltpu.VMEM((parts, edge_rows, LANES), bf16),
             pltpu.VMEM((parts, edge_rows, LANES), bf16),
             pltpu.VMEM((edge_rows, columns), jnp.float32),
-            pltpu.VMEM((edge_rows, columns), bf16),
             pltpu.VMEM((edge_rows, columns), bf16),
             pltpu.VMEM(w_edge_in.shape, bf16),
             pltpu.VMEM(w_edge_out.shape, bf16),
@@ -567,14 +572,12 @@
             pltpu.VMEM((2, share_rows // 2, columns), bf16),
             pltpu.VMEM((2, share_rows // 2, columns), bf16),
             pltpu.VMEM((2, share_rows // 2, columns), bf16),
-            pltpu.VMEM((share_rows, columns), jnp.float32),
-            pltpu.VMEM((parts, share_rows, LANES), bf16),
             pltpu.SemaphoreType.DMA((SLOTS,)),
             pltpu.SemaphoreType.DMA((SLOTS,)),
             pltpu.SemaphoreType.DMA((LOCALS,)),
         ],
         compiler_params=pltpu.CompilerParams(
-            vmem_limit_bytes=67043328, collective_id=0, has_side_effects=True
+            vmem_limit_bytes=64000000, collective_id=0, has_side_effects=True
         ),
     )(
         edge_count,
@@ -583,7 +586,7 @@
         senders.reshape(-1, LANES),
         receivers.reshape(-1, LANES),
         halo_rows,
-        coarse_rows,
+        jnp.swapaxes(coarse_rows, 1, 2),
         w_edge_in,
         row(b_edge_in),
         w_edge_out,

time: 88.4 us -> 79 us (0.89)
  Pallas kernels: 80.6 us -> 75.4 us
  local copies, waits for them, and re-layouts: 6.28 us -> 2.11 us
    pallas_call x1, Pallas kernels: 80.6 us -> 75.4 us  [layer_stage(): pl.pallas_call(lambda *refs: layer_kernel(COARSE_DEV, *refs), out_shape=(...]
    unnamed x3 -> x2, local copies, waits for them, and re-layouts: 6.28 us -> 2.11 us
where the time goes in v4:
time: 79 us; the launch traced here: 78.8 us
  Pallas kernels  75.4 us (95%)
  local copies, waits for them, and re-layouts  2.11 us (3%)
  between operations  1.29 us (2%)
    pallas_call x1, Pallas kernels, layer_stage(): pl.pallas_call(lambda *refs: layer_kernel(COARSE_DEV, *refs), out_shape=(...  75.4 us
    unnamed x2, local copies, waits for them, and re-layouts  2.11 us

profile of v4, /device:TPU:0, one launch (start us, length us, event | category | flops | bytes accessed | tf_op | source)
XLA Modules:
  0.0 78.8 jit_solution(4540051716647871646)
XLA Ops:
  1.3 75.4 %shard_map.194 = (bf16[2048,128]{1,0:T(8,128)(2,1)S(1)}, bf16[2048,512]{1,0:T(8,128)(2,1)S(1)}) custom-call(s32[1]{0:T(128)S(6)} %copy.25.refs_0_, bf16[2048,128]{1,0:T(8,128)(2,1)} %refs_1_.1, bf16[2048,512]{1,0:T(8,128)(2,1)} %refs_2_.1, s32[16,128]{1,0:T(8,128)} %bitcast.11, s32[16,128]{1,0:T(8,128)} %bitcast.12, s32[1,2,1024]{2,1,0:T(2,128)} %refs_5_.1, ...), custom_call_target="tpu_custom_call" | custom-call | tf_op jit(solution)/shard_map/pallas_call | solution.py:550
  76.7 0.8 %copy.23 = bf16[2048,128]{1,0:T(8,128)(2,1)} copy(bf16[2048,128]{1,0:T(8,128)(2,1)S(1)} %get-tuple-element.2) | data formatting | bytes 1048576
  77.5 1.3 %copy.24 = bf16[2048,512]{1,0:T(8,128)(2,1)} copy(bf16[2048,512]{1,0:T(8,128)(2,1)S(1)} %get-tuple-element.3) | data formatting | bytes 4194304

commit v5 on v4

--- a/solution.py
+++ b/solution.py
@@ -98,6 +98,7 @@
     send_sem,
     recv_sem,
     local_sem,
+    known_sem,
 ):
     edges = edges_out_ref
     p, h = lax.axis_index("patch"), lax.axis_index("hidden")
@@ -125,18 +126,13 @@
 
     barrier = pltpu.get_barrier_semaphore()
 
-    def greet(j, carry):
-        pl.semaphore_signal(
-            barrier,
-            inc=1,
-            device_id={"patch": lax.rem(p + j, patches), "hidden": h},
-            device_id_type=MESH,
-        )
-        return carry
+    def signal(sem, q, g):
+        pl.semaphore_signal(sem, inc=1, device_id={"patch": q, "hidden": g}, device_id_type=MESH)
 
     for g in (right, left, far):
-        pl.semaphore_signal(barrier, inc=1, device_id={"patch": p, "hidden": g}, device_id_type=MESH)
-    lax.fori_loop(1, patches, greet, 0)
+        signal(barrier, p, g)
+    for q in (before, after):
+        signal(barrier, q, h)
 
     nodes_in = pltpu.make_async_copy(
         nodes_ref, table.at[h, pl.ds(0, node_rows), :], local_sem.at[L_NODES]
@@ -159,7 +155,24 @@
     def loop(count, body):
         lax.fori_loop(0, count, lambda i, carry: (body(i), carry)[1], 0)
 
-    pl.semaphore_wait(barrier, patches + 2)
+    pl.semaphore_wait(barrier, shards + 1)
+
+    def tell(r):
+        for q in (lax.rem(p + 2**r, patches), lax.rem(p + patches - 2**r, patches)):
+            signal(known_sem.at[r], q, h)
+
+    def learn(r):
+        pl.semaphore_wait(known_sem.at[r], 2)
+        if r + 1 < rounds:
+            tell(r + 1)
+
+    rounds = known_sem.shape[0]
+    tell(0)
+
+    def learned(r):
+        if r < rounds:
+            learn(r)
+
     nodes_in.wait()
 
     to_right = [copy_to(rows_of(h, k), rows_of(h, k), TO_RIGHT + k, p, right) for k in range(CHUNKS)]
@@ -168,15 +181,6 @@
         to_right[a].start()
         to_left[b].start()
 
-    slot_rows = pl.ds(pl.multiple_of(p * coarse_dev, coarse_dev), coarse_dev)
-    own_coarse = table.at[h, pl.ds(0, coarse_dev), :]
-
-    def share(j, carry):
-        copy_to(own_coarse, everyone.at[slot_rows, :], COARSE, lax.rem(p + j, patches), h).start()
-        return carry
-
-    lax.fori_loop(1, patches, share, 0)
-    everyone[slot_rows, :] = own_coarse[...]
 
     long_block = min(LONG_BLOCK, edge_rows, 2 * border)
     long_lines = long_block // LANES
@@ -227,6 +231,7 @@
     middle = node_rows // 2
     halo((h,), (0,), 0, node_rows, False)
     halos[0] = send_halo((h,), (0,))
+    learned(0)
 
     edges_in.wait()
     w_in_in.wait()
@@ -249,6 +254,7 @@
         return carry
 
     lax.fori_loop(0, edge_rows // block, self_block, 0)
+    learned(1)
 
     owner = lax.broadcasted_iota(jnp.int32, (patches, LANES), 0) * coarse_dev
     spot = lax.broadcasted_iota(jnp.int32, (patches, LANES), 1)
@@ -301,9 +307,25 @@
     total_rows = table.shape[1]
     near_half(0)
     halo(near, (1, 2), 0, middle, False)
+    learned(2)
     gather(receiver_line, 0, middle, near, recv_rows, False)
+    learned(3)
+    slot_rows = pl.ds(pl.multiple_of(p * coarse_dev, coarse_dev), coarse_dev)
+    own_coarse = table.at[h, pl.ds(0, coarse_dev), :]
+
+    def share(j, carry):
+        copy_to(own_coarse, everyone.at[slot_rows, :], COARSE, lax.rem(p + j, patches), h).start()
+        return carry
+
+    lax.fori_loop(1, patches, share, 0)
+    everyone[slot_rows, :] = own_coarse[...]
+
     gather(sender_line, 0, middle, near, send_rows, False)
     near_half(1)
+    halo(near, (1, 2), middle, node_rows, True)
+    halos[1] = send_halo(near, (1, 2))
+    gather(receiver_line, middle, node_rows, near, recv_rows, True)
+    gather(sender_line, middle, node_rows, near, send_rows, True)
     peers = (patches - 1) * coarse_dev
     all_coarse = copy_to(
         everyone.at[pl.ds(0, peers), :], everyone.at[pl.ds(0, peers), :], COARSE, after, h
@@ -318,17 +340,12 @@
     for c in pick_copies:
         c.start()
 
-    halo(near, (1, 2), middle, node_rows, True)
-    halos[1] = send_halo(near, (1, 2))
-    gather(receiver_line, middle, node_rows, near, recv_rows, True)
-    gather(sender_line, middle, node_rows, near, send_rows, True)
     far_half(0)
     halo((far,), (3,), 0, middle, False)
     far_half(1)
     halo((far,), (3,), middle, node_rows, True)
     halos[2] = send_halo((far,), (3,))
     gather(receiver_line, 0, node_rows, pair, recv_rows, False)
-    gather(sender_line, 0, node_rows, pair, send_rows, False)
     for c in halos[1]:
         c.wait_recv()
     for n, g in enumerate((left, right, far)):
@@ -337,7 +354,7 @@
     gather(sender_line, node_rows, total_rows, near, send_rows, True)
     for c in halos[0] + halos[2]:
         c.wait_recv()
-    gather(sender_line, node_rows, total_rows, pair, send_rows, True)
+    gather(sender_line, 0, total_rows, pair, send_rows, False)
 
     w_out_in.wait()
 
@@ -537,6 +554,7 @@
     shards = lax.axis_size("hidden")
     patches = lax.axis_size("patch")
     share_rows = node_rows // shards
+    rounds = (patches // 2 - 1).bit_length()
     vmem = pl.BlockSpec(memory_space=pltpu.VMEM)
     smem = pl.BlockSpec(memory_space=pltpu.SMEM)
     far_away = pl.BlockSpec(memory_space=pl.ANY)
@@ -575,6 +593,7 @@
             pltpu.SemaphoreType.DMA((SLOTS,)),
             pltpu.SemaphoreType.DMA((SLOTS,)),
             pltpu.SemaphoreType.DMA((LOCALS,)),
+            pltpu.SemaphoreType.REGULAR((rounds,)),
         ],
         compiler_params=pltpu.CompilerParams(
             vmem_limit_bytes=64000000, collective_id=0, has_side_effects=True

time: 79 us -> 79.3 us (level)
  no operation moved by 1% of the time
where the time goes in v5:
time: 79.3 us; the launch traced here: 78.6 us
  Pallas kernels  75.1 us (95%)
  local copies, waits for them, and re-layouts  2.11 us (3%)
  between operations  1.29 us (2%)
    pallas_call x1, Pallas kernels, layer_stage(): pl.pallas_call(lambda *refs: layer_kernel(COARSE_DEV, *refs), out_shape=(...  75.1 us
    unnamed x2, local copies, waits for them, and re-layouts  2.11 us

profile of v5, /device:TPU:0, one launch (start us, length us, event | category | flops | bytes accessed | tf_op | source)
XLA Modules:
  0.0 78.6 jit_solution(17003354412825034227)
XLA Ops:
  1.3 75.1 %shard_map.194 = (bf16[2048,128]{1,0:T(8,128)(2,1)S(1)}, bf16[2048,512]{1,0:T(8,128)(2,1)S(1)}) custom-call(s32[1]{0:T(128)S(6)} %copy.25.refs_0_, bf16[2048,128]{1,0:T(8,128)(2,1)} %refs_1_.1, bf16[2048,512]{1,0:T(8,128)(2,1)} %refs_2_.1, s32[16,128]{1,0:T(8,128)} %bitcast.11, s32[16,128]{1,0:T(8,128)} %bitcast.12, s32[1,2,1024]{2,1,0:T(2,128)} %refs_5_.1, ...), custom_call_target="tpu_custom_call" | custom-call | tf_op jit(solution)/shard_map/pallas_call | solution.py:568
  76.4 0.8 %copy.23 = bf16[2048,128]{1,0:T(8,128)(2,1)} copy(bf16[2048,128]{1,0:T(8,128)(2,1)S(1)} %get-tuple-element.2) | data formatting | bytes 1048576
  77.2 1.3 %copy.24 = bf16[2048,512]{1,0:T(8,128)(2,1)} copy(bf16[2048,512]{1,0:T(8,128)(2,1)S(1)} %get-tuple-element.3) | data formatting | bytes 4194304

commit v6 on v5

--- a/solution.py
+++ b/solution.py
@@ -11,6 +11,10 @@
 LONG_BLOCK = 1024
 CHUNKS = 4
 MESH = pl.DeviceIdType.MESH
+
+
+def grid_of(patches):
+    return (4, 4, 2) if patches == 32 else (1, 2, patches // 2)
 
 
 layer_epsilon = 1e-05
@@ -22,7 +26,8 @@
 PLAIN_RIGHT, PLAIN_LEFT = 24 + 2 * PIECES, 24 + 3 * PIECES
 SUM_RIGHT, SUM_LEFT = 24 + 4 * PIECES, 24 + 5 * PIECES
 NEW = 24 + 6 * PIECES
-SLOTS = NEW + 6 * PIECES
+TWIN = NEW + 6 * PIECES
+SLOTS = TWIN + 1
 L_NODES, L_EDGES, L_IN, L_OUT, L_NODE_IN, L_NODE_OUT, L_RESULT, L_OWN = 0, 1, 2, 3, 4, 5, 6, 7
 LOCALS = 8
 
@@ -131,8 +136,20 @@
 
     for g in (right, left, far):
         signal(barrier, p, g)
-    for q in (before, after):
-        signal(barrier, q, h)
+    grid = grid_of(patches)
+    nearby, stride, number = [], 1, 0
+    for size in reversed(grid):
+        spot = lax.rem(lax.div(p, stride), size)
+        if size > 1:
+            nearby += [(spot > 0, p - stride), (spot < size - 1, p + stride)]
+            number = number + jnp.where(spot > 0, 1, 0) + jnp.where(spot < size - 1, 1, 0)
+        stride *= size
+
+    def tell(sem):
+        for there, q in nearby:
+            pl.when(there)(lambda q=q: signal(sem, lax.rem(q + patches, patches), h))
+
+    tell(barrier)
 
     nodes_in = pltpu.make_async_copy(
         nodes_ref, table.at[h, pl.ds(0, node_rows), :], local_sem.at[L_NODES]
@@ -155,23 +172,16 @@
     def loop(count, body):
         lax.fori_loop(0, count, lambda i, carry: (body(i), carry)[1], 0)
 
-    pl.semaphore_wait(barrier, shards + 1)
-
-    def tell(r):
-        for q in (lax.rem(p + 2**r, patches), lax.rem(p + patches - 2**r, patches)):
-            signal(known_sem.at[r], q, h)
-
-    def learn(r):
-        pl.semaphore_wait(known_sem.at[r], 2)
-        if r + 1 < rounds:
-            tell(r + 1)
+    pl.semaphore_wait(barrier, shards - 1 + number)
 
     rounds = known_sem.shape[0]
-    tell(0)
+    tell(known_sem.at[0])
 
     def learned(r):
         if r < rounds:
-            learn(r)
+            pl.semaphore_wait(known_sem.at[r], number)
+            if r + 1 < rounds:
+                tell(known_sem.at[r + 1])
 
     nodes_in.wait()
 
@@ -230,7 +240,6 @@
     edge_lines = edge_rows // LANES
     middle = node_rows // 2
     halo((h,), (0,), 0, node_rows, False)
-    halos[0] = send_halo((h,), (0,))
     learned(0)
 
     edges_in.wait()
@@ -253,10 +262,15 @@
         )
         return carry
 
-    lax.fori_loop(0, edge_rows // block, self_block, 0)
+    edge_blocks = edge_rows // block
+    lax.fori_loop(0, edge_blocks // 2, self_block, 0)
     learned(1)
-
-    owner = lax.broadcasted_iota(jnp.int32, (patches, LANES), 0) * coarse_dev
+    lax.fori_loop(edge_blocks // 2, edge_blocks, self_block, 0)
+    learned(2)
+    learned(3)
+
+    owner = lax.broadcasted_iota(jnp.int32, (patches, LANES), 0)
+    owner = (lax.rem(owner, 2) * (patches // 2) + lax.div(owner, 2)) * coarse_dev
     spot = lax.broadcasted_iota(jnp.int32, (patches, LANES), 1)
     for k in range(per_slot):
         line = coarse_ref[0, k : k + 1, :]
@@ -305,32 +319,45 @@
 
     near, pair = (left, right), (h, far)
     total_rows = table.shape[1]
+    learned(4)
+    learned(5)
+    halos[0] = send_halo((h,), (0,))
+    chips = patches // 2
+    chip, core = lax.div(p, 2), lax.rem(p, 2)
+    mine_first = pl.multiple_of((core * chips + chip) * coarse_dev, coarse_dev)
+    slot_rows = pl.ds(mine_first, coarse_dev)
+    own_coarse = table.at[h, pl.ds(0, coarse_dev), :]
+
+    def share(j, carry):
+        copy_to(own_coarse, everyone.at[slot_rows, :], COARSE, lax.rem(p + 2 * j, patches), h).start()
+        return carry
+
+    lax.fori_loop(1, chips, share, 0)
+    everyone[slot_rows, :] = own_coarse[...]
     near_half(0)
     halo(near, (1, 2), 0, middle, False)
-    learned(2)
     gather(receiver_line, 0, middle, near, recv_rows, False)
-    learned(3)
-    slot_rows = pl.ds(pl.multiple_of(p * coarse_dev, coarse_dev), coarse_dev)
-    own_coarse = table.at[h, pl.ds(0, coarse_dev), :]
-
-    def share(j, carry):
-        copy_to(own_coarse, everyone.at[slot_rows, :], COARSE, lax.rem(p + j, patches), h).start()
-        return carry
-
-    lax.fori_loop(1, patches, share, 0)
-    everyone[slot_rows, :] = own_coarse[...]
-
     gather(sender_line, 0, middle, near, send_rows, False)
     near_half(1)
     halo(near, (1, 2), middle, node_rows, True)
     halos[1] = send_halo(near, (1, 2))
     gather(receiver_line, middle, node_rows, near, recv_rows, True)
     gather(sender_line, middle, node_rows, near, send_rows, True)
-    peers = (patches - 1) * coarse_dev
+    peers = (chips - 1) * coarse_dev
     all_coarse = copy_to(
         everyone.at[pl.ds(0, peers), :], everyone.at[pl.ds(0, peers), :], COARSE, after, h
     )
     all_coarse.wait_recv()
+    group = chips * coarse_dev
+    same_core = everyone.at[pl.ds(pl.multiple_of(core * group, group), group), :]
+    to_twin = copy_to(same_core, same_core, TWIN, p + 1 - 2 * core, h)
+    to_twin.start()
+    far_half(0)
+    halo((far,), (3,), 0, middle, False)
+    far_half(1)
+    halo((far,), (3,), middle, node_rows, True)
+    halos[2] = send_halo((far,), (3,))
+    copy_to(same_core, same_core, TWIN, p + 1 - 2 * core, h).wait_recv()
     picked_rows = hot_pick.shape[0]
     picked = table.at[h, pl.ds(first_picked, picked_rows), :]
     table[h, first_picked : first_picked + picked_rows, :] = jnp.dot(
@@ -339,13 +366,8 @@
     pick_copies = [copy_to(picked, picked, PICKED + n, p, g) for n, g in enumerate((right, left, far))]
     for c in pick_copies:
         c.start()
-
-    far_half(0)
-    halo((far,), (3,), 0, middle, False)
-    far_half(1)
-    halo((far,), (3,), middle, node_rows, True)
-    halos[2] = send_halo((far,), (3,))
     gather(receiver_line, 0, node_rows, pair, recv_rows, False)
+    gather(sender_line, 0, node_rows, pair, send_rows, False)
     for c in halos[1]:
         c.wait_recv()
     for n, g in enumerate((left, right, far)):
@@ -354,16 +376,17 @@
     gather(sender_line, node_rows, total_rows, near, send_rows, True)
     for c in halos[0] + halos[2]:
         c.wait_recv()
-    gather(sender_line, 0, total_rows, pair, send_rows, False)
+    gather(sender_line, node_rows, total_rows, pair, send_rows, True)
 
     w_out_in.wait()
 
     def edge_block(i, carry):
         start = pl.multiple_of(i * block, block)
         here = pl.ds(start, block)
+        parts = range(columns // LANES)
         gathered = jnp.concatenate(
-            [send_rows[c, here, :] for c in range(columns // LANES)]
-            + [recv_rows[c, here, :] for c in range(columns // LANES)],
+            [send_rows[c, here, :] for c in parts]
+            + [recv_rows[c, here, :] for c in parts],
             axis=1,
         )
         value = pre[here, :] + jnp.dot(
@@ -515,6 +538,7 @@
     for c in halos[0] + halos[1] + halos[2]:
         c.wait_send()
     all_coarse.wait_send()
+    to_twin.wait_send()
     for c in ring + plain_right + plain_left + sum_copies + new_copies:
         c.wait_send()
     for k in range(PIECES):
@@ -554,7 +578,7 @@
     shards = lax.axis_size("hidden")
     patches = lax.axis_size("patch")
     share_rows = node_rows // shards
-    rounds = (patches // 2 - 1).bit_length()
+    rounds = sum(grid_of(patches)) - 4
     vmem = pl.BlockSpec(memory_space=pltpu.VMEM)
     smem = pl.BlockSpec(memory_space=pltpu.SMEM)
     far_away = pl.BlockSpec(memory_space=pl.ANY)

time: 79.3 us -> 75.4 us (0.951)
  Pallas kernels: 75.1 us -> 71.8 us
    pallas_call x1, Pallas kernels: 75.1 us -> 71.8 us  [layer_stage(): pl.pallas_call(lambda *refs: layer_kernel(COARSE_DEV, *refs), out_shape=(...]
where the time goes in v6:
time: 75.4 us; the launch traced here: 75.2 us
  Pallas kernels  71.8 us (95%)
  local copies, waits for them, and re-layouts  2.11 us (3%)
  between operations  1.29 us (2%)
    pallas_call x1, Pallas kernels, layer_stage(): pl.pallas_call(lambda *refs: layer_kernel(COARSE_DEV, *refs), out_shape=(...  71.8 us
    unnamed x2, local copies, waits for them, and re-layouts  2.11 us

profile of v6, /device:TPU:0, one launch (start us, length us, event | category | flops | bytes accessed | tf_op | source)
XLA Modules:
  0.0 75.2 jit_solution(18436994038473415675)
XLA Ops:
  1.3 71.8 %shard_map.194 = (bf16[2048,128]{1,0:T(8,128)(2,1)S(1)}, bf16[2048,512]{1,0:T(8,128)(2,1)S(1)}) custom-call(s32[1]{0:T(128)S(6)} %copy.25.refs_0_, bf16[2048,128]{1,0:T(8,128)(2,1)} %refs_1_.1, bf16[2048,512]{1,0:T(8,128)(2,1)} %refs_2_.1, s32[16,128]{1,0:T(8,128)} %bitcast.11, s32[16,128]{1,0:T(8,128)} %bitcast.12, s32[1,2,1024]{2,1,0:T(2,128)} %refs_5_.1, ...), custom_call_target="tpu_custom_call" | custom-call | tf_op jit(solution)/shard_map/pallas_call | solution.py:592
  73.1 0.8 %copy.23 = bf16[2048,128]{1,0:T(8,128)(2,1)} copy(bf16[2048,128]{1,0:T(8,128)(2,1)S(1)} %get-tuple-element.2) | data formatting | bytes 1048576
  73.9 1.3 %copy.24 = bf16[2048,512]{1,0:T(8,128)(2,1)} copy(bf16[2048,512]{1,0:T(8,128)(2,1)S(1)} %get-tuple-element.3) | data formatting | bytes 4194304

commit v7 on v6

--- a/solution.py
+++ b/solution.py
@@ -319,7 +319,10 @@
 
     near, pair = (left, right), (h, far)
     total_rows = table.shape[1]
+    near_half(0)
+    halo(near, (1, 2), 0, middle, False)
     learned(4)
+    gather(receiver_line, 0, middle, near, recv_rows, False)
     learned(5)
     halos[0] = send_halo((h,), (0,))
     chips = patches // 2
@@ -334,15 +337,14 @@
 
     lax.fori_loop(1, chips, share, 0)
     everyone[slot_rows, :] = own_coarse[...]
-    near_half(0)
-    halo(near, (1, 2), 0, middle, False)
-    gather(receiver_line, 0, middle, near, recv_rows, False)
     gather(sender_line, 0, middle, near, send_rows, False)
     near_half(1)
     halo(near, (1, 2), middle, node_rows, True)
     halos[1] = send_halo(near, (1, 2))
     gather(receiver_line, middle, node_rows, near, recv_rows, True)
     gather(sender_line, middle, node_rows, near, send_rows, True)
+    far_half(0)
+    halo((far,), (3,), 0, middle, False)
     peers = (chips - 1) * coarse_dev
     all_coarse = copy_to(
         everyone.at[pl.ds(0, peers), :], everyone.at[pl.ds(0, peers), :], COARSE, after, h
@@ -352,8 +354,6 @@
     same_core = everyone.at[pl.ds(pl.multiple_of(core * group, group), group), :]
     to_twin = copy_to(same_core, same_core, TWIN, p + 1 - 2 * core, h)
     to_twin.start()
-    far_half(0)
-    halo((far,), (3,), 0, middle, False)
     far_half(1)
     halo((far,), (3,), middle, node_rows, True)
     halos[2] = send_halo((far,), (3,))

time: 75.4 us -> 76.7 us (1.017)
  Pallas kernels: 71.8 us -> 72.8 us
    pallas_call x1, Pallas kernels: 71.8 us -> 72.8 us  [layer_stage(): pl.pallas_call(lambda *refs: layer_kernel(COARSE_DEV, *refs), out_shape=(...]
where the time goes in v7:
time: 76.7 us; the launch traced here: 76.2 us
  Pallas kernels  72.8 us (95%)
  local copies, waits for them, and re-layouts  2.11 us (3%)
  between operations  1.29 us (2%)
    pallas_call x1, Pallas kernels, layer_stage(): pl.pallas_call(lambda *refs: layer_kernel(COARSE_DEV, *refs), out_shape=(...  72.8 us
    unnamed x2, local copies, waits for them, and re-layouts  2.11 us

profile of v7, /device:TPU:0, one launch (start us, length us, event | category | flops | bytes accessed | tf_op | source)
XLA Modules:
  0.0 76.2 jit_solution(13897942199754361287)
XLA Ops:
  1.3 72.8 %shard_map.194 = (bf16[2048,128]{1,0:T(8,128)(2,1)S(1)}, bf16[2048,512]{1,0:T(8,128)(2,1)S(1)}) custom-call(s32[1]{0:T(128)S(6)} %copy.25.refs_0_, bf16[2048,128]{1,0:T(8,128)(2,1)} %refs_1_.1, bf16[2048,512]{1,0:T(8,128)(2,1)} %refs_2_.1, s32[16,128]{1,0:T(8,128)} %bitcast.11, s32[16,128]{1,0:T(8,128)} %bitcast.12, s32[1,2,1024]{2,1,0:T(2,128)} %refs_5_.1, ...), custom_call_target="tpu_custom_call" | custom-call | tf_op jit(solution)/shard_map/pallas_call | solution.py:592
  74.1 0.8 %copy.23 = bf16[2048,128]{1,0:T(8,128)(2,1)} copy(bf16[2048,128]{1,0:T(8,128)(2,1)S(1)} %get-tuple-element.2) | data formatting | bytes 1048576
  74.9 1.3 %copy.24 = bf16[2048,512]{1,0:T(8,128)(2,1)} copy(bf16[2048,512]{1,0:T(8,128)(2,1)S(1)} %get-tuple-element.3) | data formatting | bytes 4194304
